TPU v7x, 32 devices: a whole 2x2x4 slice. The times are simulated.
32 devices in a mesh: blk: 16 (over z, y, core), tp: 2 (over x).
Axes of the slice: x: 2, y: 2, z: 4, core: 2. Of those that a mesh axis runs over, the one named last changes fastest.
Arguments:
- dec_states: bfloat16 [4096, 5120], P('blk', 'tp'), may hold values from -200 to 200
- norm_gain: float32 [5120], replicated, may hold values from 0.1 to 1.9
- query_weight: bfloat16 [5120, 768], P(None, 'tp'), may hold values from -0.078125 to 0.078125
- out_weight: bfloat16 [768, 5120], P('tp'), may hold values from -0.21875 to 0.21875
- enc_keys: bfloat16 [6144, 768], P('blk', 'tp'), may hold values from -1000 to 1000
- enc_values: bfloat16 [6144, 768], P('blk', 'tp'), may hold values from -6 to 6
Outputs:
- attn_out: bfloat16 [4096, 5120], P('blk', 'tp')
All inputs are finite; a program needn't handle non-finite values.
Results may differ from a plain program's by a relative error of at most 0.034.
Values may be sent and summed in bfloat16 or wider, within the bound.
A program may use at most 128 MiB of HBM per device.

v0:
```python
import functools
import math

import jax
import jax.numpy as jnp
from jax import lax
from jax.experimental import pallas as pl
from jax.experimental.pallas import tpu as pltpu
from jax.sharding import PartitionSpec as P

HEAD_DIM = 128
NORM_EPS = 1e-06
LANES = 128


def column_tile(width, limit=640):
    best = LANES
    for tile in range(LANES, limit + 1, LANES):
        if width % tile == 0:
            best = tile
    return best


def kernel(
    n_blk,
    n_tp,
    x_hbm,
    gain_ref,
    wq_hbm,
    wo_hbm,
    k_hbm,
    v_hbm,
    out_hbm,
    kvbuf,
    wq,
    wo,
    xbuf,
    xg,
    qsend,
    qrecv,
    own_part,
    sqbuf,
    qbuf,
    attbuf,
    oacc,
    obuf,
    kv_send,
    kv_recv,
    move_send,
    tp_send,
    tp_recv,
    head_send,
    head_recv,
    sib_send,
    sib_recv,
    kv_local,
    wo_local,
    local_sem,
    out_sem,
):
    n_line = n_blk // 4
    b = lax.axis_index("blk")
    t = lax.axis_index("tp")
    core = lax.rem(b, 2)
    side = lax.rem(lax.div(b, 2), 2)
    line = lax.div(b, 4)
    rows = x_hbm.shape[0]
    feat = x_hbm.shape[1]
    width = wq_hbm.shape[1]
    heads = width // HEAD_DIM
    pieces = 2 * heads
    half_feat = feat // 2
    half_head = HEAD_DIM // 2
    moved = ()
    ahead = 3

    def index(zz, yy, cc):
        return (zz * 2 + yy) * 2 + cc

    sibling = index(line, side, 1 - core)
    beside = index(line, 1 - side, core)
    peers = [lax.rem(t + off, n_tp) for off in range(1, n_tp)]

    def ds(start, size, mult=LANES):
        return pl.ds(pl.multiple_of(start, mult), size)

    def head_cols(h):
        return slice(h * HEAD_DIM, (h + 1) * HEAD_DIM)

    kv_loads = [
        pltpu.make_async_copy(
            (k_hbm, v_hbm)[e % 2].at[:, head_cols(e // 2)], kvbuf.at[e, b], kv_local.at[e]
        )
        for e in range(pieces)
    ]
    wo_loads = [
        pltpu.make_async_copy(
            wo_hbm.at[head_cols(h), ds(t * feat, feat)], wo.at[t, h], wo_local.at[h]
        )
        for h in range(heads)
    ]
    x_load = pltpu.make_async_copy(x_hbm, xbuf, local_sem.at[0])
    wq_load = pltpu.make_async_copy(wq_hbm.at[ds(t * feat, feat)], wq.at[t], local_sem.at[1])
    for load in kv_loads + [x_load, wq_load] + wo_loads:
        load.start()

    barrier = pltpu.get_barrier_semaphore()
    has_left = line > 0
    has_right = line < n_line - 1

    @pl.when(has_left)
    def _():
        pl.semaphore_signal(barrier, inc=1, device_id={"blk": b - 4})

    @pl.when(has_right)
    def _():
        pl.semaphore_signal(barrier, inc=1, device_id={"blk": b + 4})

    pl.semaphore_signal(barrier, inc=1, device_id={"blk": sibling})
    pl.semaphore_signal(barrier, inc=1, device_id={"blk": beside})
    for p in peers:
        pl.semaphore_signal(barrier, inc=1, device_id={"tp": p})
    ends = jnp.where(has_left, 1, 0) + jnp.where(has_right, 1, 0)
    pl.semaphore_wait(barrier, 2 + len(peers) + ends)

    def kv_copy(e, send_sem, slot, target):
        return pltpu.make_async_remote_copy(
            src_ref=kvbuf.at[e, slot],
            dst_ref=kvbuf.at[e, slot],
            send_sem=send_sem,
            recv_sem=kv_recv.at[e, slot],
            device_id={"blk": target},
        )

    def right_copy(e, zz):
        return kv_copy(e, kv_send.at[e, 0, zz], index(zz, side, core), b + 4)

    def left_copy(e, zz):
        return kv_copy(e, kv_send.at[e, 1, zz], index(zz, side, core), b - 4)

    def beside_copy(e, zz):
        return kv_copy(e, kv_send.at[e, 2, zz], index(zz, side, core), beside)

    def sib_copy(e, zz):
        return kv_copy(e, kv_send.at[e, 3, zz], index(zz, side, core), sibling)

    def sib_beside_copy(e, zz):
        return kv_copy(e, kv_send.at[e, 4, zz], index(zz, 1 - side, core), sibling)

    def move_left(e):
        return kv_copy(e, move_send.at[0, e], index(n_line - 1, 1 - side, core), b - 4)

    def move_right(e):
        return kv_copy(e, move_send.at[1, e], index(0, 1 - side, core), b + 4)

    def goes_beside(e, zz):
        inner = (zz > 0) & (zz < n_line - 1)
        return inner | (zz == line) if e in moved else zz >= 0

    def wait_slot(e, slot):
        kv_copy(e, kv_send.at[e, 0, 0], slot, sibling).wait_recv()

    def own_event(e):
        if e >= pieces:
            return
        kv_loads[e].wait()

        @pl.when(has_left)
        def _():
            left_copy(e, line).start()

        @pl.when(has_right)
        def _():
            right_copy(e, line).start()

        beside_copy(e, line).start()
        sib_copy(e, line).start()

    def column_event(e, d):
        @pl.when(line + d < n_line)
        def _():
            zz = line + d
            wait_slot(e, index(zz, side, core))

            @pl.when(has_left)
            def _():
                left_copy(e, zz).start()

            @pl.when(goes_beside(e, zz))
            def _():
                beside_copy(e, zz).start()

            sib_copy(e, zz).start()

        @pl.when(line - d >= 0)
        def _():
            zz = line - d
            wait_slot(e, index(zz, side, core))

            @pl.when(has_right)
            def _():
                right_copy(e, zz).start()

            @pl.when(goes_beside(e, zz))
            def _():
                beside_copy(e, zz).start()

            sib_copy(e, zz).start()

    def move_event(e, d):
        @pl.when(line + d == n_line - 1)
        def _():
            zz = line + d
            wait_slot(e, index(zz, 1 - side, core))

            @pl.when(has_left)
            def _():
                move_left(e).start()

            sib_beside_copy(e, zz).start()

        @pl.when(line - d == 0)
        def _():
            zz = line - d
            wait_slot(e, index(zz, 1 - side, core))

            @pl.when(has_right)
            def _():
                move_right(e).start()

            sib_beside_copy(e, zz).start()

    def nearest(k):
        short = jnp.minimum(line, n_line - 1 - line)
        swing = line + (k + 1) // 2 if k % 2 == 1 else line - k // 2
        tail = jnp.where(line < n_line - 1 - line, k, n_line - 1 - k)
        return jnp.where(k <= 2 * short, swing, tail)

    def beside_event(e, k):
        zz = nearest(k)

        def handle():
            wait_slot(e, index(zz, 1 - side, core))
            sib_beside_copy(e, zz).start()

        if e in moved:
            pl.when((zz > 0) & (zz < n_line - 1))(handle)
        else:
            handle()

    def wave(s):
        for d in range(1, n_line):
            e = s + 1 - d
            if 0 <= e < pieces:
                column_event(e, d)
        own_event(s + ahead)
        for d in range(n_line):
            if s - d in moved:
                move_event(s - d, d)

    n_waves = pieces + n_line - 2

    def tp_copy(src, dst, send_sem, recv_sem, p):
        return pltpu.make_async_remote_copy(
            src_ref=src, dst_ref=dst, send_sem=send_sem, recv_sem=recv_sem, device_id={"tp": p}
        )

    def wq_half(p, cc):
        return wq.at[p, ds(cc * half_feat, half_feat)]

    def wq_copy(i, p):
        src = wq_hbm.at[ds(p * feat + core * half_feat, half_feat)]
        return tp_copy(src, wq_half(t, core), tp_send.at[0, i], tp_recv.at[0, t], p)

    def wq_landed(p):
        ref = wq_half(p, core)
        return tp_copy(ref, ref, tp_send.at[0, 0], tp_recv.at[0, p], p)

    def wq_sib(p, cc):
        return pltpu.make_async_remote_copy(
            src_ref=wq_half(p, cc),
            dst_ref=wq_half(p, cc),
            send_sem=sib_send.at[heads, p],
            recv_sem=sib_recv.at[heads, p],
            device_id={"blk": sibling},
        )

    def wo_half(p, h, cc):
        return wo.at[p, h, ds(cc * half_head, half_head, half_head)]

    def wo_copy(i, p, h):
        src = wo_hbm.at[ds(h * HEAD_DIM + core * half_head, half_head, half_head), ds(p * feat, feat)]
        return tp_copy(src, wo_half(t, h, core), head_send.at[0, h, i], head_recv.at[0, h, t], p)

    def wo_landed(p, h):
        ref = wo_half(p, h, core)
        return tp_copy(ref, ref, head_send.at[0, h, 0], head_recv.at[0, h, p], p)

    def wo_sib(p, h, cc):
        return pltpu.make_async_remote_copy(
            src_ref=wo_half(p, h, cc),
            dst_ref=wo_half(p, h, cc),
            send_sem=sib_send.at[h, p],
            recv_sem=sib_recv.at[h, p],
            device_id={"blk": sibling},
        )

    def sq_copy(i, p, slot):
        ref = sqbuf.at[slot]
        return tp_copy(ref, ref, tp_send.at[1, i], tp_recv.at[1, slot], p)

    def q_copy(i, p, slot):
        return tp_copy(qsend.at[p], qrecv.at[slot], tp_send.at[2, i], tp_recv.at[2, slot], p)

    def att_copy(i, p, h, slot):
        ref = attbuf.at[slot, h]
        return tp_copy(ref, ref, head_send.at[1, h, i], head_recv.at[1, h, slot], p)

    for i, p in enumerate(peers):
        wq_copy(i, p).start()
    for e in range(ahead):
        own_event(e)

    x_load.wait()
    tile = column_tile(feat)
    squares = jnp.zeros((rows, 1), jnp.float32)
    for start in range(0, feat, tile):
        piece = xbuf[:, start : start + tile].astype(jnp.float32)
        squares += jnp.sum(piece * piece, axis=1, keepdims=True)
        gain = gain_ref[:, ds(t * feat + start, tile)]
        xg[:, start : start + tile] = (piece * gain).astype(jnp.bfloat16)
    wide = jnp.broadcast_to(squares, (rows, LANES))
    sqbuf[t] = jnp.transpose(wide)[0:8, :]
    wave(0)
    wq_load.wait()
    own_part[...] = jnp.dot(xg[...], wq[t], preferred_element_type=jnp.float32)
    for i, p in enumerate(peers):
        sq_copy(i, p, t).start()
    weights_wave = n_waves // 2
    for s in range(1, weights_wave):
        wave(s)

    for p in peers:
        wq_landed(p).wait_recv()
        wq_sib(p, core).start()
    for i, p in enumerate(peers):
        wq_sib(p, 1 - core).wait_recv()
        qsend[p] = jnp.dot(xg[...], wq[p], preferred_element_type=jnp.float32).astype(
            jnp.bfloat16
        )
        q_copy(i, p, t).start()
    for h in range(heads - 1):
        for i, p in enumerate(peers):
            wo_copy(i, p, h).start()

    wave(weights_wave)

    total = sqbuf[t][0:1, :]
    for i, p in enumerate(peers):
        sq_copy(i, p, p).wait_recv()
        total = total + sqbuf[p][0:1, :]
    column = jnp.transpose(jnp.broadcast_to(total, (LANES, rows)))
    scale = math.log2(math.e) / math.sqrt(HEAD_DIM)
    factor = lax.rsqrt(column / (feat * n_tp) + NORM_EPS) * scale
    for i, p in enumerate(peers):
        q_copy(i, p, p).wait_recv()
    for h in range(heads):
        summed = own_part[:, head_cols(h)]
        for p in peers:
            summed = summed + qrecv[p, :, head_cols(h)].astype(jnp.float32)
        qbuf[:, head_cols(h)] = (summed * factor).astype(jnp.bfloat16)

    def attend(h, state, zz, yy):
        for e in (2 * h, 2 * h + 1):
            wait_slot(e, index(zz, yy, 1 - core))
        first = index(zz, yy, 0)
        keys = kvbuf[2 * h, pl.ds(first, 2)].reshape(-1, HEAD_DIM)
        vals = kvbuf[2 * h + 1, pl.ds(first, 2)].reshape(-1, HEAD_DIM)
        scores = lax.dot_general(
            qbuf[:, head_cols(h)],
            keys,
            (((1,), (1,)), ((), ())),
            preferred_element_type=jnp.float32,
        )
        old, row_sum, acc = state
        new = jnp.maximum(old, jnp.max(scores, axis=1, keepdims=True))
        weights = jnp.exp2(scores - new)
        keep = jnp.exp2(old - new)
        row_sum = row_sum * keep + jnp.sum(weights, axis=1, keepdims=True)
        mixed = jnp.dot(weights.astype(jnp.bfloat16), vals, preferred_element_type=jnp.float32)
        return new, row_sum, acc * keep + mixed

    def head_attention(h):
        state = (
            jnp.full((rows, 1), -1e30, jnp.float32),
            jnp.zeros((rows, 1), jnp.float32),
            jnp.zeros((rows, HEAD_DIM), jnp.float32),
        )
        for e in (2 * h, 2 * h + 1):
            beside_event(e, 0)
        for k in range(n_line):
            state = attend(h, state, nearest(k), side)
            if k >= 1:
                state = attend(h, state, nearest(k - 1), 1 - side)
            if k + 1 < n_line:
                for e in (2 * h, 2 * h + 1):
                    beside_event(e, k + 1)
        unused, row_sum, acc = attend(h, state, nearest(n_line - 1), 1 - side)
        attbuf[t, h] = (acc / row_sum).astype(jnp.bfloat16)
        for i, p in enumerate(peers):
            att_copy(i, p, h, t).start()

    done = weights_wave + 1
    for h in range(heads):
        need = n_waves if h == heads - 1 else min(2 * h + 1 + n_line, n_waves)
        while done < need:
            wave(done)
            done += 1
        for hh in range(heads - 1):
            if h == heads - 1:
                for p in peers:
                    wo_landed(p, hh).wait_recv()
                    wo_sib(p, hh, core).start()
        head_attention(h)
        if h == 0:
            for i, p in enumerate(peers):
                wo_copy(i, p, heads - 1).start()

    last = heads - 1
    for p in peers:
        wo_landed(p, last).wait_recv()
        wo_sib(p, last, core).start()
    for load in wo_loads:
        load.wait()
    for h in range(heads - 1):
        for i, p in enumerate(peers):
            wo_sib(p, h, 1 - core).wait_recv()
            att_copy(i, p, h, p).wait_recv()
    starts = range(0, feat, tile)
    for start in starts:
        cols = slice(start, start + tile)
        result = jnp.dot(attbuf[t, last], wo[t, last, :, cols], preferred_element_type=jnp.float32)
        for p in range(n_tp):
            for h in range(heads - 1):
                result += jnp.dot(
                    attbuf[p, h], wo[p, h, :, cols], preferred_element_type=jnp.float32
                )
        oacc[:, cols] = result
    for i, p in enumerate(peers):
        wo_sib(p, last, 1 - core).wait_recv()
        att_copy(i, p, last, p).wait_recv()
    stores = []
    for j, start in enumerate(starts):
        cols = slice(start, start + tile)
        result = oacc[:, cols]
        for p in peers:
            result += jnp.dot(
                attbuf[p, last], wo[p, last, :, cols], preferred_element_type=jnp.float32
            )
        obuf[:, cols] = result.astype(jnp.bfloat16)
        store = pltpu.make_async_copy(obuf.at[:, cols], out_hbm.at[:, cols], out_sem.at[j])
        store.start()
        stores.append(store)

    for e in range(pieces):
        for zz in range(n_line):

            @pl.when(has_right & (line >= zz))
            def _():
                right_copy(e, zz).wait_send()

            @pl.when(has_left & (line <= zz))
            def _():
                left_copy(e, zz).wait_send()

            if e in moved and zz in (0, n_line - 1):

                @pl.when(line == zz)
                def _():
                    beside_copy(e, zz).wait_send()

            else:
                beside_copy(e, zz).wait_send()
            sib_copy(e, zz).wait_send()
            sib_beside_copy(e, zz).wait_send()
        if e in moved:

            @pl.when(has_left)
            def _():
                move_left(e).wait_send()

            @pl.when(has_right)
            def _():
                move_right(e).wait_send()

    for i, p in enumerate(peers):
        wq_copy(i, p).wait_send()
        sq_copy(i, p, t).wait_send()
        q_copy(i, p, t).wait_send()
        wq_sib(p, core).wait_send()
        for h in range(heads):
            wo_copy(i, p, h).wait_send()
            att_copy(i, p, h, t).wait_send()
            wo_sib(p, h, core).wait_send()
    for store in stores:
        store.wait()


def per_device(n_blk, n_tp, dec_states, norm_gain, query_weight, out_weight, enc_keys, enc_values):
    rows, feat = dec_states.shape
    width = query_weight.shape[1]
    enc_rows = enc_keys.shape[0]
    heads = width // HEAD_DIM
    n_line = n_blk // 4
    tiles = feat // column_tile(feat)
    bf16, f32 = jnp.bfloat16, jnp.float32
    dma = pltpu.SemaphoreType.DMA
    anywhere = pl.BlockSpec(memory_space=pl.ANY)
    return pl.pallas_call(
        functools.partial(kernel, n_blk, n_tp),
        out_shape=jax.ShapeDtypeStruct((rows, feat), bf16),
        in_specs=[
            anywhere,
            pl.BlockSpec(memory_space=pltpu.VMEM),
            anywhere,
            anywhere,
            anywhere,
            anywhere,
        ],
        out_specs=anywhere,
        scratch_shapes=[
            pltpu.VMEM((2 * heads, n_blk, enc_rows, HEAD_DIM), bf16),
            pltpu.VMEM((n_tp, feat, width), bf16),
            pltpu.VMEM((n_tp, heads, HEAD_DIM, feat), bf16),
            pltpu.VMEM((rows, feat), bf16),
            pltpu.VMEM((rows, feat), bf16),
            pltpu.VMEM((n_tp, rows, width), bf16),
            pltpu.VMEM((n_tp, rows, width), bf16),
            pltpu.VMEM((rows, width), f32),
            pltpu.VMEM((n_tp, 8, rows), f32),
            pltpu.VMEM((rows, width), bf16),
            pltpu.VMEM((n_tp, heads, rows, HEAD_DIM), bf16),
            pltpu.VMEM((rows, feat), f32),
            pltpu.VMEM((rows, feat), bf16),
            dma((2 * heads, 5, n_line)),
            dma((2 * heads, n_blk)),
            dma((2, 2 * heads)),
            dma((3, n_tp)),
            dma((3, n_tp)),
            dma((2, heads, n_tp)),
            dma((2, heads, n_tp)),
            dma((heads + 1, n_tp)),
            dma((heads + 1, n_tp)),
            dma((2 * heads,)),
            dma((heads,)),
            dma((2,)),
            dma((tiles,)),
        ],
        compiler_params=pltpu.CompilerParams(
            collective_id=0, has_side_effects=True, vmem_limit_bytes=60 * 1024 * 1024
        ),
    )(dec_states, norm_gain.reshape(1, -1), query_weight, out_weight, enc_keys, enc_values)


def solution(mesh):
    in_specs = (P("blk", "tp"), P(), P(None, "tp"), P("tp", None), P("blk", "tp"), P("blk", "tp"))
    out_specs = P("blk", "tp")
    body = functools.partial(per_device, mesh.shape["blk"], mesh.shape["tp"])
    return jax.shard_map(body, mesh=mesh, in_specs=in_specs, out_specs=out_specs, check_vma=False)
```

profile of v0, /device:TPU:0, one launch (start us, length us, event | category | flops | bytes accessed | tf_op | source)
XLA Modules:
  0.0 69.9 jit_solution(16974327047016193631)
XLA Ops:
  0.0 67.4 %shard_map.64 = bf16[256,2560]{1,0:T(8,128)(2,1)} custom-call(bf16[256,2560]{1,0:T(8,128)(2,1)} %x_hbm.1, f32[1,5120]{1,0:T(1,128)} %bitcast.1, bf16[5120,384]{1,0:T(8,128)(2,1)} %wq_hbm.1, bf16[384,5120]{1,0:T(8,128)(2,1)} %wo_hbm.1, bf16[384,384]{1,0:T(8,128)(2,1)} %k_hbm.1, bf16[384,384]{1,0:T(8,128)(2,1)} %v_hbm.1), custom_call_target="tpu_custom_call" | custom-call | tf_op jit(solution)/shard_map/pallas_call | solution.py:519
  67.4 2.5 %copy.8 = bf16[256,2560]{1,0:T(8,128)(2,1)} copy(bf16[256,2560]{1,0:T(8,128)(2,1)} %shard_map.64) | data formatting | bytes 2621440
where the time goes:
time: 70.1 us; the launch traced here: 69.9 us
  Pallas kernels  67.4 us (96%)
  local copies, waits for them, and re-layouts  2.46 us (4%)
    pallas_call x1, Pallas kernels, per_device(): pl.pallas_call(functools.partial(kernel, n_blk, n_tp), out_shape=jax.Shap...  67.4 us
    unnamed x1, local copies, waits for them, and re-layouts  2.46 us

commit v1 on v0

v1 whole, which is shorter than its diff:
```python
import functools
import math

import jax
import jax.numpy as jnp
from jax import lax
from jax.experimental import pallas as pl
from jax.experimental.pallas import tpu as pltpu
from jax.sharding import PartitionSpec as P

HEAD_DIM = 128
NORM_EPS = 1e-06
LANES = 128
SUBS = 2


def column_tile(width, limit=640):
    best = LANES
    for tile in range(LANES, limit + 1, LANES):
        if width % tile == 0:
            best = tile
    return best


def kernel(
    n_blk,
    n_tp,
    x_hbm,
    gain_ref,
    wq_hbm,
    wo_hbm,
    k_hbm,
    v_hbm,
    out_hbm,
    kvbuf,
    wq_own,
    wq,
    wo,
    xbuf,
    xg,
    qsend,
    qrecv,
    own_part,
    sqbuf,
    fbuf,
    qbuf,
    qmate,
    osend,
    orecv,
    ssend,
    srecv,
    opart,
    lse_own,
    att,
    oacc,
    obuf,
    kv_send,
    kv_recv,
    wq_send,
    wq_recv,
    wo_send,
    wo_recv,
    sq_send,
    sq_recv,
    head_send,
    head_recv,
    mate_send,
    mate_recv,
    kv_local,
    local_sem,
    out_sem,
):
    n_line = n_blk // 4
    n_pair = n_line // 2
    b = lax.axis_index("blk")
    t = lax.axis_index("tp")
    core = lax.rem(b, 2)
    side = lax.rem(lax.div(b, 2), 2)
    line = lax.div(b, 4)
    par = lax.rem(line, 2)
    pair = lax.div(line, 2)
    rows = x_hbm.shape[0]
    feat = x_hbm.shape[1]
    width = wq_hbm.shape[1]
    heads = width // HEAD_DIM
    span = n_tp * HEAD_DIM
    last = heads - 1
    wq_rows = feat // (4 * SUBS)
    wo_rows = HEAD_DIM // 4

    def index(zz, yy, cc):
        return (zz * 2 + yy) * 2 + cc

    sibling = index(line, side, 1 - core)
    beside = index(line, 1 - side, core)
    partner = index(line + 1 - 2 * par, side, core)
    peers = [lax.rem(t + off, n_tp) for off in range(1, n_tp)]
    mates = [lax.rem(pair + off, n_pair) for off in range(1, n_pair)]

    def mate_index(m):
        return index(2 * m + par, side, core)

    def ds(start, size, mult=LANES):
        return pl.ds(pl.multiple_of(start, mult), size)

    def head_cols(h):
        return slice(h * HEAD_DIM, (h + 1) * HEAD_DIM)

    def slot(pp, yy, cc):
        return (pp * 2 + yy) * 2 + cc

    mine = slot(par, side, core)

    kv_loads = [
        pltpu.make_async_copy(
            (k_hbm, v_hbm)[e % 2].at[:, head_cols(e // 2)], kvbuf.at[e, mine], kv_local.at[e]
        )
        for e in range(2 * heads)
    ]
    x_load = pltpu.make_async_copy(x_hbm, xbuf, local_sem.at[0])
    wq_load = pltpu.make_async_copy(wq_hbm.at[ds(t * feat, feat)], wq_own, local_sem.at[1])
    wo_loads = [
        pltpu.make_async_copy(
            wo_hbm.at[head_cols(h), ds(t * feat, feat)],
            wo.at[ds(h * span + t * HEAD_DIM, HEAD_DIM)],
            local_sem.at[2 + h],
        )
        for h in range(heads)
    ]
    for load in kv_loads[:2] + [x_load, wq_load] + kv_loads[2:] + wo_loads:
        load.start()

    barrier = pltpu.get_barrier_semaphore()
    for other in [sibling, beside, partner] + [mate_index(m) for m in mates]:
        pl.semaphore_signal(barrier, inc=1, device_id={"blk": other})
    for p in peers:
        pl.semaphore_signal(barrier, inc=1, device_id={"tp": p})
    pl.semaphore_wait(barrier, 3 + len(mates) + len(peers))

    sends = []

    def remote(src, dst, send_sem, recv_sem, device_id):
        return pltpu.make_async_remote_copy(
            src_ref=src, dst_ref=dst, send_sem=send_sem, recv_sem=recv_sem, device_id=device_id
        )

    def launch(copy):
        copy.start()
        sends.append(copy)

    def kv_copy(e, s, k, target):
        ref = kvbuf.at[e, s]
        return remote(ref, ref, kv_send.at[e, k], kv_recv.at[e, s], {"blk": target})

    def kv_wait(e, s):
        kv_copy(e, s, 0, sibling).wait_recv()

    from_beside = slot(par, 1 - side, core)
    from_partner = slot(1 - par, side, core)
    from_corner = slot(1 - par, 1 - side, core)

    def kv_own(h):
        for e in (2 * h, 2 * h + 1):
            kv_loads[e].wait()
            launch(kv_copy(e, mine, 1, partner))
            launch(kv_copy(e, mine, 0, beside))
            launch(kv_copy(e, mine, 3, sibling))

    def kv_pass(h):
        for e in (2 * h, 2 * h + 1):
            kv_wait(e, from_partner)
            launch(kv_copy(e, from_partner, 2, beside))
            launch(kv_copy(e, from_partner, 4, sibling))
            kv_wait(e, from_beside)
            launch(kv_copy(e, from_beside, 5, sibling))

    def kv_corner(h):
        for e in (2 * h, 2 * h + 1):
            kv_wait(e, from_corner)
            launch(kv_copy(e, from_corner, 6, sibling))

    def kv_ready(h):
        for e in (2 * h, 2 * h + 1):
            for pp, yy in ((par, side), (par, 1 - side), (1 - par, side), (1 - par, 1 - side)):
                kv_wait(e, slot(pp, yy, 1 - core))

    def wq_chunk(pp, cc, sub):
        return (pp * 2 + cc) * SUBS + sub

    def wq_ref(p, h, c):
        return wq.at[p, h, ds(c * wq_rows, wq_rows, 16)]

    def wq_hop(p, h, c, k, target):
        ref = wq_ref(p, h, c)
        return remote(ref, ref, wq_send.at[p, h, k], wq_recv.at[p, h, c], {"blk": target})

    def wq_wait(p, h, c):
        wq_hop(p, h, c, 0, sibling).wait_recv()

    def wq_start(h):
        for sub in range(SUBS):
            for p in peers:
                c = wq_chunk(par, core, sub)
                src = wq_hbm.at[ds(p * feat + c * wq_rows, wq_rows, 16), head_cols(h)]
                launch(
                    remote(
                        src, wq_ref(t, h, c), wq_send.at[p, h, sub], wq_recv.at[t, h, c], {"tp": p}
                    )
                )

    def wq_pass(h):
        for sub in range(SUBS):
            for p in peers:
                c = wq_chunk(par, core, sub)
                wq_wait(p, h, c)
                launch(wq_hop(p, h, c, SUBS + sub, partner))
                launch(wq_hop(p, h, c, 2 * SUBS + sub, sibling))

    def wq_relay(h):
        for sub in range(SUBS):
            for p in peers:
                c = wq_chunk(1 - par, core, sub)
                wq_wait(p, h, c)
                launch(wq_hop(p, h, c, 3 * SUBS + sub, sibling))

    def q_copy(p, h, s):
        return remote(
            qsend.at[p, h], qrecv.at[s, h], head_send.at[0, p, h], head_recv.at[0, s, h], {"tp": p}
        )

    def q_part(h):
        for p in peers:
            for pp in (par, 1 - par):
                for sub in range(SUBS):
                    wq_wait(p, h, wq_chunk(pp, 1 - core, sub))
            qsend[p, h] = jnp.dot(
                xg[...], wq[p, h], preferred_element_type=jnp.float32
            ).astype(jnp.bfloat16)
            launch(q_copy(p, h, t))

    def sq_copy(p, s):
        ref = sqbuf.at[s]
        return remote(ref, ref, sq_send.at[p], sq_recv.at[s], {"tp": p})

    tile = column_tile(feat)

    def norm():
        x_load.wait()
        squares = jnp.zeros((rows, 1), jnp.float32)
        for start in range(0, feat, tile):
            piece = xbuf[:, start : start + tile].astype(jnp.float32)
            squares += jnp.sum(piece * piece, axis=1, keepdims=True)
            gain = gain_ref[:, ds(t * feat + start, tile)]
            xg[:, start : start + tile] = (piece * gain).astype(jnp.bfloat16)
        wide = jnp.broadcast_to(squares, (rows, LANES))
        sqbuf[t] = jnp.transpose(wide)[0:8, :]
        for p in peers:
            launch(sq_copy(p, t))
        wq_load.wait()
        own_part[...] = jnp.dot(xg[...], wq_own[...], preferred_element_type=jnp.float32)

    def factor():
        total = sqbuf[t][0:1, :]
        for p in peers:
            sq_copy(p, p).wait_recv()
            total = total + sqbuf[p][0:1, :]
        column = jnp.transpose(jnp.broadcast_to(total, (LANES, rows)))
        scale = math.log2(math.e) / math.sqrt(HEAD_DIM)
        fbuf[...] = lax.rsqrt(column / (feat * n_tp) + NORM_EPS) * scale

    def mate_copy(k, src, dst, h, m, s):
        return remote(
            src, dst, mate_send.at[k, h, m], mate_recv.at[k, h, s], {"blk": mate_index(m)}
        )

    def mq_copy(h, m, s):
        return mate_copy(0, qbuf.at[h], qmate.at[h, s], h, m, s)

    def mo_copy(h, m, s):
        return mate_copy(1, osend.at[h, m], orecv.at[h, s], h, m, s)

    def ms_copy(h, m, s):
        return mate_copy(2, ssend.at[h, m], srecv.at[h, s], h, m, s)

    def q_make(h):
        summed = own_part[:, head_cols(h)]
        for p in peers:
            q_copy(p, h, p).wait_recv()
            summed = summed + qrecv[p, h].astype(jnp.float32)
        qbuf[h] = (summed * fbuf[...]).astype(jnp.bfloat16)
        for m in mates:
            launch(mq_copy(h, m, pair))

    def attend(h, query):
        scores = []
        for i in range(4):
            keys = kvbuf[2 * h, 2 * i : 2 * i + 2].reshape(-1, HEAD_DIM)
            scores.append(
                lax.dot_general(
                    query, keys, (((1,), (1,)), ((), ())), preferred_element_type=jnp.float32
                )
            )
        top = scores[0]
        for s in scores[1:]:
            top = jnp.maximum(top, s)
        top = jnp.max(top, axis=1, keepdims=True)
        mixed = jnp.zeros((rows, 2 * HEAD_DIM), jnp.float32)
        for i in range(4):
            vals = kvbuf[2 * h + 1, 2 * i : 2 * i + 2].reshape(-1, HEAD_DIM)
            wide = jnp.concatenate([vals, jnp.ones_like(vals)], axis=1)
            weights = jnp.exp2(scores[i] - top).astype(jnp.bfloat16)
            mixed = mixed + jnp.dot(weights, wide, preferred_element_type=jnp.float32)
        total = mixed[:, HEAD_DIM:]
        return mixed[:, :HEAD_DIM] / total, top + jnp.log(total) * math.log2(math.e)

    def att_own(h):
        opart[h], lse_own[h] = attend(h, qbuf[h])

    def att_mate(h):
        for m in mates:
            mq_copy(h, m, m).wait_recv()
            out, lse = attend(h, qmate[h, m])
            osend[h, m] = out.astype(jnp.bfloat16)
            launch(mo_copy(h, m, pair))
            ssend[h, m] = jnp.transpose(lse)[0:8, :]
            launch(ms_copy(h, m, pair))

    def att_cols(p, h):
        return att.at[:, ds(h * span + p * HEAD_DIM, HEAD_DIM)]

    def att_copy(p, h, s):
        ref = att_cols(s, h)
        return remote(ref, ref, head_send.at[1, p, h], head_recv.at[1, s, h], {"tp": p})

    def merge(h):
        parts = [opart[h]]
        logs = [lse_own[h]]
        for m in mates:
            mo_copy(h, m, m).wait_recv()
            ms_copy(h, m, m).wait_recv()
            parts.append(orecv[h, m].astype(jnp.float32))
            logs.append(jnp.transpose(jnp.broadcast_to(srecv[h, m][0:1, :], (LANES, rows))))
        top = logs[0]
        for log in logs[1:]:
            top = jnp.maximum(top, log)
        shares = [jnp.exp2(log - top) for log in logs]
        total = shares[0]
        mixed = shares[0] * parts[0]
        for share, part in zip(shares[1:], parts[1:]):
            total = total + share
            mixed = mixed + share * part
        att[:, ds(h * span + t * HEAD_DIM, HEAD_DIM)] = (mixed / total).astype(jnp.bfloat16)
        for p in peers:
            launch(att_copy(p, h, t))

    def wo_ref(p, h, q):
        return wo.at[ds(h * span + p * HEAD_DIM + q * wo_rows, wo_rows, wo_rows)]

    def wo_hop(p, h, q, k, target):
        ref = wo_ref(p, h, q)
        return remote(ref, ref, wo_send.at[p, h, k], wo_recv.at[p, h, q], {"blk": target})

    def wo_wait(p, h, q):
        wo_hop(p, h, q, 0, sibling).wait_recv()

    def wo_start(h):
        q = side * 2 + core
        for p in peers:
            src = wo_hbm.at[ds(h * HEAD_DIM + q * wo_rows, wo_rows, wo_rows), ds(p * feat, feat)]
            launch(
                remote(src, wo_ref(t, h, q), wo_send.at[p, h, 0], wo_recv.at[t, h, q], {"tp": p})
            )

    def wo_pass(h):
        for p in peers:
            q = side * 2 + core
            wo_wait(p, h, q)
            launch(wo_hop(p, h, q, 1, beside))
            launch(wo_hop(p, h, q, 2, sibling))

    def wo_relay(h):
        for p in peers:
            q = (1 - side) * 2 + core
            wo_wait(p, h, q)
            launch(wo_hop(p, h, q, 3, sibling))

    def wo_ready(h):
        wo_loads[h].wait()
        for p in peers:
            for yy in (side, 1 - side):
                wo_wait(p, h, yy * 2 + 1 - core)

    starts = range(0, feat, tile)

    def project_most():
        for h in range(last):
            wo_ready(h)
            for p in peers:
                att_copy(p, h, p).wait_recv()
        for start in starts:
            cols = slice(start, start + tile)
            oacc[:, cols] = jnp.dot(
                att[:, : last * span], wo[: last * span, cols], preferred_element_type=jnp.float32
            )

    events = []

    def at(when, step, *args):
        events.append((when, len(events), step, args))

    for h in range(heads):
        at(2.0 + 0.1 * h, wq_start, h)
        at(2.5 + 6.0 * h, kv_own, h)
        at(6.5 + 3.6 * h, wq_pass, h)
        at(7.0 + 7.0 * h, kv_pass, h)
        at(10.2 + 3.9 * h, wq_relay, h)
        at(11.5 + 6.5 * h, kv_corner, h)
        at(13.0 + 3.6 * h, q_part, h)
        at(16.7 + 3.8 * h, q_make, h)
        at(17.0 + 3.8 * h, kv_ready, h)
        at(17.2 + 3.8 * h, att_own, h)
        at(21.7 + 3.9 * h, att_mate, h)
        at((13.1 if h == 0 else 20.3) + 0.01 * h, wo_start, h)
        at(26.0 + 3.0 * h, wo_pass, h)
        at(32.5 + 0.1 * h, wo_relay, h)
        at(33.0 + 2.0 * h, merge, h)
    at(4.0, norm)
    at(16.0, factor)
    at(36.0, project_most)
    for when, order, step, args in sorted(events, key=lambda event: event[:2]):
        step(*args)

    wo_ready(last)
    for p in peers:
        att_copy(p, last, p).wait_recv()
    stores = []
    for j, start in enumerate(starts):
        cols = slice(start, start + tile)
        result = oacc[:, cols] + jnp.dot(
            att[:, last * span :], wo[last * span :, cols], preferred_element_type=jnp.float32
        )
        obuf[:, cols] = result.astype(jnp.bfloat16)
        store = pltpu.make_async_copy(obuf.at[:, cols], out_hbm.at[:, cols], out_sem.at[j])
        store.start()
        stores.append(store)
    for copy in sends:
        copy.wait_send()
    for store in stores:
        store.wait()


def per_device(n_blk, n_tp, dec_states, norm_gain, query_weight, out_weight, enc_keys, enc_values):
    rows, feat = dec_states.shape
    width = query_weight.shape[1]
    enc_rows = enc_keys.shape[0]
    heads = width // HEAD_DIM
    n_pair = n_blk // 8
    tiles = feat // column_tile(feat)
    bf16, f32 = jnp.bfloat16, jnp.float32
    dma = pltpu.SemaphoreType.DMA
    anywhere = pl.BlockSpec(memory_space=pl.ANY)
    return pl.pallas_call(
        functools.partial(kernel, n_blk, n_tp),
        out_shape=jax.ShapeDtypeStruct((rows, feat), bf16),
        in_specs=[
            anywhere,
            pl.BlockSpec(memory_space=pltpu.VMEM),
            anywhere,
            anywhere,
            anywhere,
            anywhere,
        ],
        out_specs=anywhere,
        scratch_shapes=[
            pltpu.VMEM((2 * heads, 8, enc_rows, HEAD_DIM), bf16),
            pltpu.VMEM((feat, width), bf16),
            pltpu.VMEM((n_tp, heads, feat, HEAD_DIM), bf16),
            pltpu.VMEM((n_tp * width, feat), bf16),
            pltpu.VMEM((rows, feat), bf16),
            pltpu.VMEM((rows, feat), bf16),
            pltpu.VMEM((n_tp, heads, rows, HEAD_DIM), bf16),
            pltpu.VMEM((n_tp, heads, rows, HEAD_DIM), bf16),
            pltpu.VMEM((rows, width), f32),
            pltpu.VMEM((n_tp, 8, rows), f32),
            pltpu.VMEM((rows, LANES), f32),
            pltpu.VMEM((heads, rows, HEAD_DIM), bf16),
            pltpu.VMEM((heads, n_pair, rows, HEAD_DIM), bf16),
            pltpu.VMEM((heads, n_pair, rows, HEAD_DIM), bf16),
            pltpu.VMEM((heads, n_pair, rows, HEAD_DIM), bf16),
            pltpu.VMEM((heads, n_pair, 8, rows), f32),
            pltpu.VMEM((heads, n_pair, 8, rows), f32),
            pltpu.VMEM((heads, rows, HEAD_DIM), f32),
            pltpu.VMEM((heads, rows, LANES), f32),
            pltpu.VMEM((rows, n_tp * width), bf16),
            pltpu.VMEM((rows, feat), f32),
            pltpu.VMEM((rows, feat), bf16),
            dma((2 * heads, 7)),
            dma((2 * heads, 8)),
            dma((n_tp, heads, 4 * SUBS)),
            dma((n_tp, heads, 4 * SUBS)),
            dma((n_tp, heads, 4)),
            dma((n_tp, heads, 4)),
            dma((n_tp,)),
            dma((n_tp,)),
            dma((2, n_tp, heads)),
            dma((2, n_tp, heads)),
            dma((3, heads, n_pair)),
            dma((3, heads, n_pair)),
            dma((2 * heads,)),
            dma((2 + heads,)),
            dma((tiles,)),
        ],
        compiler_params=pltpu.CompilerParams(
            collective_id=0, has_side_effects=True, vmem_limit_bytes=60 * 1024 * 1024
        ),
    )(dec_states, norm_gain.reshape(1, -1), query_weight, out_weight, enc_keys, enc_values)


def solution(mesh):
    in_specs = (P("blk", "tp"), P(), P(None, "tp"), P("tp", None), P("blk", "tp"), P("blk", "tp"))
    out_specs = P("blk", "tp")
    body = functools.partial(per_device, mesh.shape["blk"], mesh.shape["tp"])
    return jax.shard_map(body, mesh=mesh, in_specs=in_specs, out_specs=out_specs, check_vma=False)
```

time: 70.1 us -> 71.3 us (1.017)
  Pallas kernels: 67.4 us -> 68.7 us
    pallas_call x1, Pallas kernels: 67.4 us -> 68.7 us  [per_device(): pl.pallas_call(functools.partial(kernel, n_blk, n_tp), out_shape=jax.Shap...]
where the time goes in v1:
time: 71.3 us; the launch traced here: 71.1 us
  Pallas kernels  68.7 us (96%)
  local copies, waits for them, and re-layouts  2.46 us (3%)
    pallas_call x1, Pallas kernels, per_device(): pl.pallas_call(functools.partial(kernel, n_blk, n_tp), out_shape=jax.Shap...  68.7 us
    unnamed x1, local copies, waits for them, and re-layouts  2.46 us

profile of v1, /device:TPU:0, one launch (start us, length us, event | category | flops | bytes accessed | tf_op | source)
XLA Modules:
  0.0 71.1 jit_solution(18212304516548954958)
XLA Ops:
  0.0 68.7 %shard_map.64 = bf16[256,2560]{1,0:T(8,128)(2,1)} custom-call(bf16[256,2560]{1,0:T(8,128)(2,1)} %x_hbm.1, f32[1,5120]{1,0:T(1,128)} %bitcast.1, bf16[5120,384]{1,0:T(8,128)(2,1)} %wq_hbm.1, bf16[384,5120]{1,0:T(8,128)(2,1)} %wo_hbm.1, bf16[384,384]{1,0:T(8,128)(2,1)} %k_hbm.1, bf16[384,384]{1,0:T(8,128)(2,1)} %v_hbm.1), custom_call_target="tpu_custom_call" | custom-call | tf_op jit(solution)/shard_map/pallas_call | solution.py:462
  68.7 2.5 %copy.8 = bf16[256,2560]{1,0:T(8,128)(2,1)} copy(bf16[256,2560]{1,0:T(8,128)(2,1)} %shard_map.64) | data formatting | bytes 2621440

commit v2 on v1

v2 whole, which is shorter than its diff:
```python
import functools
import math

import jax
import jax.numpy as jnp
from jax import lax
from jax.experimental import pallas as pl
from jax.experimental.pallas import tpu as pltpu
from jax.sharding import PartitionSpec as P

HEAD_DIM = 128
NORM_EPS = 1e-06
LANES = 128
SUBS = 2


def column_tile(width, limit=640):
    best = LANES
    for tile in range(LANES, limit + 1, LANES):
        if width % tile == 0:
            best = tile
    return best


def kernel(
    n_blk,
    n_tp,
    x_hbm,
    gain_hbm,
    wq_hbm,
    wo_hbm,
    k_hbm,
    v_hbm,
    out_ref,
    gain_ref,
    kvbuf,
    wq_own,
    wq,
    wo,
    xbuf,
    xg,
    qsend,
    qrecv,
    own_part,
    sqbuf,
    fbuf,
    qbuf,
    qmate,
    osend,
    orecv,
    ssend,
    srecv,
    opart,
    lse_own,
    att,
    oacc,
    send_sem,
    kv_recv,
    kv_core_recv,
    wq_recv,
    wq_core_recv,
    wo_recv,
    wo_core_recv,
    sq_recv,
    head_recv,
    mate_recv,
    kv_local,
    local_sem,
):
    n_line = n_blk // 4
    n_pair = n_line // 2
    b = lax.axis_index("blk")
    t = lax.axis_index("tp")
    core = lax.rem(b, 2)
    side = lax.rem(lax.div(b, 2), 2)
    line = lax.div(b, 4)
    par = lax.rem(line, 2)
    pair = lax.div(line, 2)
    rows = x_hbm.shape[0]
    feat = x_hbm.shape[1]
    width = wq_hbm.shape[1]
    heads = width // HEAD_DIM
    span = n_tp * HEAD_DIM
    last = heads - 1
    wq_rows = feat // (4 * SUBS)
    wo_rows = HEAD_DIM // (4 * SUBS)

    def index(zz, yy, cc):
        return (zz * 2 + yy) * 2 + cc

    sibling = index(line, side, 1 - core)
    beside = index(line, 1 - side, core)
    partner = index(line + 1 - 2 * par, side, core)
    peers = [lax.rem(t + off, n_tp) for off in range(1, n_tp)]
    mates = [lax.rem(pair + off, n_pair) for off in range(1, n_pair)]
    n_peer, n_mate = len(peers), len(mates)

    def mate_index(m):
        return index(2 * m + par, side, core)

    def ds(start, size, mult=LANES):
        return pl.ds(pl.multiple_of(start, mult), size)

    def head_cols(h):
        return slice(h * HEAD_DIM, (h + 1) * HEAD_DIM)

    def slot(pp, yy, cc):
        return (pp * 2 + yy) * 2 + cc

    mine = slot(par, side, core)

    kv_loads = [
        pltpu.make_async_copy(
            (k_hbm, v_hbm)[e % 2].at[:, head_cols(e // 2)], kvbuf.at[e, mine], kv_local.at[e // 2]
        )
        for e in range(2 * heads)
    ]
    x_load = pltpu.make_async_copy(x_hbm, xbuf, local_sem.at[0])
    gain_load = pltpu.make_async_copy(gain_hbm, gain_ref, local_sem.at[3])
    wq_load = pltpu.make_async_copy(wq_hbm.at[ds(t * feat, feat)], wq_own, local_sem.at[1])
    wo_loads = [
        pltpu.make_async_copy(
            wo_hbm.at[head_cols(h), ds(t * feat, feat)],
            wo.at[ds(h * span + t * HEAD_DIM, HEAD_DIM)],
            local_sem.at[2],
        )
        for h in range(heads)
    ]
    for load in kv_loads[:2] + [gain_load, x_load, wq_load] + kv_loads[2:] + wo_loads:
        load.start()

    barrier = pltpu.get_barrier_semaphore()
    for other in [sibling, beside, partner] + [mate_index(m) for m in mates]:
        pl.semaphore_signal(barrier, inc=1, device_id={"blk": other})
    for p in peers:
        pl.semaphore_signal(barrier, inc=1, device_id={"tp": p})
    pl.semaphore_wait(barrier, 3 + len(mates) + len(peers))

    def remote(src, dst, kind, recv_sem, device_id):
        return pltpu.make_async_remote_copy(
            src_ref=src,
            dst_ref=dst,
            send_sem=send_sem.at[kind],
            recv_sem=recv_sem,
            device_id=device_id,
        )

    def arrived(ref, recv_sem):
        remote(ref, ref, 0, recv_sem, {"blk": sibling}).wait_recv()

    def sent(ref, kind):
        remote(ref, ref, kind, kv_core_recv.at[0], {"blk": sibling}).wait_send()

    def kv_send(e, s, kind, target):
        ref = kvbuf.at[e, s]
        remote(ref, ref, 0, kv_recv.at[e, kind], {"blk": target}).start()

    def kv_share(e, s):
        ref = kvbuf.at[e, s]
        remote(ref, ref, 0, kv_core_recv.at[e // 2], {"blk": sibling}).start()

    def kv_wait(e, s, kind):
        arrived(kvbuf.at[e, s], kv_recv.at[e, kind])

    from_beside = slot(par, 1 - side, core)
    from_partner = slot(1 - par, side, core)
    from_corner = slot(1 - par, 1 - side, core)

    by_line = (2 * heads - 1,)

    def kv_loaded(h):
        both = kvbuf.at[2 * h : 2 * h + 2, mine]
        pltpu.make_async_copy(both, both, kv_local.at[h]).wait()

    def kv_line(e):
        kv_send(e, mine, 1, partner)

    def kv_side(e):
        kv_send(e, mine, 0, beside)

    def kv_core(e):
        kv_share(e, mine)

    def kv_from_partner(e):
        kv_wait(e, from_partner, 1)
        if e not in by_line:
            kv_send(e, from_partner, 2, beside)
        kv_share(e, from_partner)

    def kv_from_beside(e):
        kv_wait(e, from_beside, 0)
        if e in by_line:
            kv_send(e, from_beside, 2, partner)
        kv_share(e, from_beside)

    def kv_from_corner(e):
        kv_wait(e, from_corner, 2)
        kv_share(e, from_corner)

    def kv_ready(h):
        arrived(kvbuf.at[2 * h : 2 * h + 2, 0:4], kv_core_recv.at[h])

    def wq_chunk(pp, cc, sub):
        return (pp * 2 + cc) * SUBS + sub

    def wq_ref(p, h, c):
        return wq.at[p, h, ds(c * wq_rows, wq_rows, 16)]

    def wq_hop(j, h, c, k):
        ref = wq_ref(peers[j], h, c)
        remote(ref, ref, 1, wq_recv.at[j, h, k], {"blk": partner}).start()

    def wq_share(j, h, c):
        ref = wq_ref(peers[j], h, c)
        remote(ref, ref, 1, wq_core_recv.at[j, h], {"blk": sibling}).start()

    def wq_start(h):
        for k in range(2 * SUBS if h == last else SUBS):
            for j, p in enumerate(peers):
                c = wq_chunk(par if k < SUBS else 1 - par, core, k % SUBS)
                src = wq_hbm.at[ds(p * feat + c * wq_rows, wq_rows, 16), head_cols(h)]
                place = wq_recv.at[n_peer - 1 - j, h, k]
                remote(src, wq_ref(t, h, c), 1, place, {"tp": p}).start()

    def wq_pass(h, sub):
        for j, p in enumerate(peers):
            c = wq_chunk(par, core, sub)
            arrived(wq_ref(p, h, c), wq_recv.at[j, h, sub])
            if h != last:
                wq_hop(j, h, c, SUBS + sub)
            wq_share(j, h, c)

    def wq_relay(h, sub):
        for j, p in enumerate(peers):
            c = wq_chunk(1 - par, core, sub)
            arrived(wq_ref(p, h, c), wq_recv.at[j, h, SUBS + sub])
            wq_share(j, h, c)

    def q_part(h):
        for j, p in enumerate(peers):
            arrived(wq.at[p, h, 0 : feat // 2], wq_core_recv.at[j, h])
            qsend[p, h] = jnp.dot(
                xg[...], wq[p, h], preferred_element_type=jnp.float32
            ).astype(jnp.bfloat16)
            place = head_recv.at[0, n_peer - 1 - j, h]
            remote(qsend.at[p, h], qrecv.at[t, h], 3, place, {"tp": p}).start()

    tile = column_tile(feat)

    def norm():
        gain_load.wait()
        x_load.wait()
        squares = jnp.zeros((rows, 1), jnp.float32)
        for start in range(0, feat, tile):
            piece = xbuf[:, start : start + tile].astype(jnp.float32)
            squares += jnp.sum(piece * piece, axis=1, keepdims=True)
            gain = gain_ref[:, ds(t * feat + start, tile)]
            xg[:, start : start + tile] = (piece * gain).astype(jnp.bfloat16)
        wide = jnp.broadcast_to(squares, (rows, LANES))
        sqbuf[t] = jnp.transpose(wide)[0:8, :]
        for j, p in enumerate(peers):
            ref = sqbuf.at[t]
            remote(ref, ref, 2, sq_recv.at[n_peer - 1 - j], {"tp": p}).start()
        wq_load.wait()
        own_part[...] = jnp.dot(xg[...], wq_own[...], preferred_element_type=jnp.float32)

    def factor():
        total = sqbuf[t][0:1, :]
        for j, p in enumerate(peers):
            arrived(sqbuf.at[p], sq_recv.at[j])
            total = total + sqbuf[p][0:1, :]
        column = jnp.transpose(jnp.broadcast_to(total, (LANES, rows)))
        scale = math.log2(math.e) / math.sqrt(HEAD_DIM)
        fbuf[...] = lax.rsqrt(column / (feat * n_tp) + NORM_EPS) * scale

    def mate_send(k, src, dst, h, i):
        place = mate_recv.at[k, h, n_mate - 1 - i]
        remote(src, dst, 5 + k, place, {"blk": mate_index(mates[i])}).start()

    def q_make(h):
        summed = own_part[:, head_cols(h)]
        for j, p in enumerate(peers):
            arrived(qrecv.at[p, h], head_recv.at[0, j, h])
            summed = summed + qrecv[p, h].astype(jnp.float32)
        qbuf[h] = (summed * fbuf[...]).astype(jnp.bfloat16)
        for i in range(n_mate):
            mate_send(0, qbuf.at[h], qmate.at[h, pair], h, i)

    def attend(h, query):
        scores = []
        for i in range(4):
            keys = kvbuf[2 * h, 2 * i : 2 * i + 2].reshape(-1, HEAD_DIM)
            scores.append(
                lax.dot_general(
                    query, keys, (((1,), (1,)), ((), ())), preferred_element_type=jnp.float32
                )
            )
        top = scores[0]
        for s in scores[1:]:
            top = jnp.maximum(top, s)
        top = jnp.max(top, axis=1, keepdims=True)
        mixed = jnp.zeros((rows, 2 * HEAD_DIM), jnp.float32)
        for i in range(4):
            vals = kvbuf[2 * h + 1, 2 * i : 2 * i + 2].reshape(-1, HEAD_DIM)
            wide = jnp.concatenate([vals, jnp.ones_like(vals)], axis=1)
            weights = jnp.exp2(scores[i] - top).astype(jnp.bfloat16)
            mixed = mixed + jnp.dot(weights, wide, preferred_element_type=jnp.float32)
        total = mixed[:, HEAD_DIM:]
        return mixed[:, :HEAD_DIM] / total, top + jnp.log(total) * math.log2(math.e)

    def att_own(h):
        opart[h], lse_own[h] = attend(h, qbuf[h])

    def att_mate(h):
        for i, m in enumerate(mates):
            arrived(qmate.at[h, m], mate_recv.at[0, h, i])
            out, lse = attend(h, qmate[h, m])
            osend[h, m] = out.astype(jnp.bfloat16)
            mate_send(1, osend.at[h, m], orecv.at[h, pair], h, i)
            ssend[h, m] = jnp.transpose(lse)[0:8, :]
            mate_send(2, ssend.at[h, m], srecv.at[h, pair], h, i)

    def att_cols(p, h):
        return att.at[:, ds(h * span + p * HEAD_DIM, HEAD_DIM)]

    def merge(h):
        parts = [opart[h]]
        logs = [lse_own[h]]
        for i, m in enumerate(mates):
            arrived(orecv.at[h, m], mate_recv.at[1, h, i])
            arrived(srecv.at[h, m], mate_recv.at[2, h, i])
            parts.append(orecv[h, m].astype(jnp.float32))
            logs.append(jnp.transpose(jnp.broadcast_to(srecv[h, m][0:1, :], (LANES, rows))))
        top = logs[0]
        for log in logs[1:]:
            top = jnp.maximum(top, log)
        shares = [jnp.exp2(log - top) for log in logs]
        total = shares[0]
        mixed = shares[0] * parts[0]
        for share, part in zip(shares[1:], parts[1:]):
            total = total + share
            mixed = mixed + share * part
        att[:, ds(h * span + t * HEAD_DIM, HEAD_DIM)] = (mixed / total).astype(jnp.bfloat16)
        for j, p in enumerate(peers):
            place = head_recv.at[1, n_peer - 1 - j, h]
            remote(att_cols(t, h), att_cols(t, h), 4, place, {"tp": p}).start()

    def att_wait(h):
        for j, p in enumerate(peers):
            arrived(att_cols(p, h), head_recv.at[1, j, h])

    def wo_ref(p, h, q):
        return wo.at[ds(h * span + p * HEAD_DIM + q * wo_rows, wo_rows, wo_rows)]

    def wo_chunk(yy, cc, sub):
        return (yy * 2 + cc) * SUBS + sub

    def wo_start(h, sub):
        q = wo_chunk(side, core, sub)
        for j, p in enumerate(peers):
            src = wo_hbm.at[ds(h * HEAD_DIM + q * wo_rows, wo_rows, wo_rows), ds(p * feat, feat)]
            place = wo_recv.at[n_peer - 1 - j, h, sub]
            remote(src, wo_ref(t, h, q), 8, place, {"tp": p}).start()

    def wo_pass(h, sub):
        for j, p in enumerate(peers):
            ref = wo_ref(p, h, wo_chunk(side, core, sub))
            arrived(ref, wo_recv.at[j, h, sub])
            remote(ref, ref, 8, wo_recv.at[j, h, SUBS + sub], {"blk": beside}).start()
            remote(ref, ref, 8, wo_core_recv.at[j, h], {"blk": sibling}).start()

    def wo_relay(h, sub):
        for j, p in enumerate(peers):
            ref = wo_ref(p, h, wo_chunk(1 - side, core, sub))
            arrived(ref, wo_recv.at[j, h, SUBS + sub])
            remote(ref, ref, 8, wo_core_recv.at[j, h], {"blk": sibling}).start()

    def wo_loaded():
        ref = wo.at[0:width]
        pltpu.make_async_copy(ref, ref, local_sem.at[2]).wait()

    def wo_ready(h):
        for j in range(n_peer):
            arrived(wo.at[0 : HEAD_DIM // 2], wo_core_recv.at[j, h])

    starts = range(0, feat, tile)

    def project_most():
        wo_loaded()
        for h in range(last):
            wo_ready(h)
            att_wait(h)
        for start in starts:
            cols = slice(start, start + tile)
            oacc[:, cols] = jnp.dot(
                att[:, : last * span], wo[: last * span, cols], preferred_element_type=jnp.float32
            )

    events = []

    def at(when, step, *args):
        events.append((when, len(events), step, args))

    for h in range(heads):
        k, v = 2 * h, 2 * h + 1
        stage = max(h - last + 2, 0)
        at(2.0 + 0.1 * h, wq_start, h)
        at(2.45 if h == 0 else 2.6 + 0.01 * h, kv_loaded, h)
        for e in (k, v):
            at(2.5 + 0.01 * e if h == 0 else 12.0 + 0.01 * e, kv_line, e)
            at(2.5 + 0.01 * e if h == 0 else 2.65 if h < last else 9.0, kv_side, e)
            at(2.7 + 0.01 * e, kv_core, e)
        at((6.5, 17.7, 21.9)[stage], kv_from_partner, k)
        at((8.6, 19.8, 24.0)[stage], kv_from_partner, v)
        at((8.7, 12.9, 21.3)[stage], kv_from_beside, k)
        at((8.8, 13.0, 21.4)[stage], kv_from_beside, v)
        at((15.0, 23.3, 26.9)[stage], kv_from_corner, k)
        at((17.0, 24.6, 26.95)[stage], kv_from_corner, v)
        for sub in range(SUBS):
            at((6.4, 9.9, 14.1)[stage] + 1.75 * sub, wq_pass, h, sub)
            at((12.0, 15.6, 17.6)[stage] + (1.75 if h == last else 0.2) * sub, wq_relay, h, sub)
            at(17.5 if stage == 0 and sub == 0 else 21.2 + 0.1 * h, wo_start, h, sub)
            at((26.8, 29.1, 31.6)[stage], wo_pass, h, sub)
            at((31.7, 35.2, 37.1)[stage], wo_relay, h, sub)
        at((13.6, 17.2, 20.7)[stage], q_part, h)
        at((19.8, 22.0, 24.5)[stage], q_make, h)
        at((21.3, 26.98, 29.2)[stage], kv_ready, h)
        at((21.4, 31.8, 33.5)[stage], att_own, h)
        at((24.8, 27.0, 29.5)[stage], att_mate, h)
        at((31.75, 35.0, 37.0)[stage], merge, h)
    at(4.0, norm)
    at(19.7, factor)
    at(37.5, project_most)
    for when, order, step, args in sorted(events, key=lambda event: event[:2]):
        with jax.named_scope("_".join([step.__name__] + [str(a) for a in args])):
            step(*args)

    with jax.named_scope("tail_wait"):
        wo_ready(last)
        att_wait(last)
    for start in starts:
        cols = slice(start, start + tile)
        result = oacc[:, cols] + jnp.dot(
            att[:, last * span :], wo[last * span :, cols], preferred_element_type=jnp.float32
        )
        out_ref[:, cols] = result.astype(jnp.bfloat16)
    with jax.named_scope("drain"):
        sent(kvbuf.at[:, 0:7], 0)
        if n_peer:
            sent(wq.at[0:n_peer], 1)
            sent(sqbuf.at[0:n_peer], 2)
            sent(qsend.at[0:n_peer], 3)
            sent(qsend.at[0:n_peer], 4)
            sent(wo.at[0 : n_peer * width], 8)
        if n_mate:
            sent(qmate.at[:, 0:n_mate], 5)
            sent(osend.at[:, 0:n_mate], 6)
            sent(ssend.at[:, 0:n_mate], 7)


def per_device(n_blk, n_tp, dec_states, norm_gain, query_weight, out_weight, enc_keys, enc_values):
    rows, feat = dec_states.shape
    width = query_weight.shape[1]
    enc_rows = enc_keys.shape[0]
    heads = width // HEAD_DIM
    n_pair = n_blk // 8
    bf16, f32 = jnp.bfloat16, jnp.float32
    dma = pltpu.SemaphoreType.DMA
    anywhere = pl.BlockSpec(memory_space=pl.ANY)
    return pl.pallas_call(
        functools.partial(kernel, n_blk, n_tp),
        out_shape=pltpu.VMEM((rows, feat), bf16),
        in_specs=[
            anywhere,
            anywhere,
            anywhere,
            anywhere,
            anywhere,
            anywhere,
        ],
        out_specs=pl.BlockSpec(memory_space=pltpu.VMEM),
        scratch_shapes=[
            pltpu.VMEM((1, n_tp * feat), f32),
            pltpu.VMEM((2 * heads, 8, enc_rows, HEAD_DIM), bf16),
            pltpu.VMEM((feat, width), bf16),
            pltpu.VMEM((n_tp, heads, feat, HEAD_DIM), bf16),
            pltpu.VMEM((n_tp * width, feat), bf16),
            pltpu.VMEM((rows, feat), bf16),
            pltpu.VMEM((rows, feat), bf16),
            pltpu.VMEM((n_tp, heads, rows, HEAD_DIM), bf16),
            pltpu.VMEM((n_tp, heads, rows, HEAD_DIM), bf16),
            pltpu.VMEM((rows, width), f32),
            pltpu.VMEM((n_tp, 8, rows), f32),
            pltpu.VMEM((rows, LANES), f32),
            pltpu.VMEM((heads, rows, HEAD_DIM), bf16),
            pltpu.VMEM((heads, n_pair, rows, HEAD_DIM), bf16),
            pltpu.VMEM((heads, n_pair, rows, HEAD_DIM), bf16),
            pltpu.VMEM((heads, n_pair, rows, HEAD_DIM), bf16),
            pltpu.VMEM((heads, n_pair, 8, rows), f32),
            pltpu.VMEM((heads, n_pair, 8, rows), f32),
            pltpu.VMEM((heads, rows, HEAD_DIM), f32),
            pltpu.VMEM((heads, rows, LANES), f32),
            pltpu.VMEM((rows, n_tp * width), bf16),
            pltpu.VMEM((rows, feat), f32),
            dma((9,)),
            dma((2 * heads, 3)),
            dma((heads,)),
            dma((n_tp - 1, heads, 2 * SUBS)),
            dma((n_tp - 1, heads)),
            dma((n_tp - 1, heads, 2 * SUBS)),
            dma((n_tp - 1, heads)),
            dma((n_tp - 1,)),
            dma((2, n_tp - 1, heads)),
            dma((3, heads, max(n_pair - 1, 1))),
            dma((heads,)),
            dma((4,)),
        ],
        compiler_params=pltpu.CompilerParams(
            collective_id=0, has_side_effects=True, vmem_limit_bytes=60 * 1024 * 1024
        ),
    )(dec_states, norm_gain.reshape(1, -1), query_weight, out_weight, enc_keys, enc_values)


def solution(mesh):
    in_specs = (P("blk", "tp"), P(), P(None, "tp"), P("tp", None), P("blk", "tp"), P("blk", "tp"))
    out_specs = P("blk", "tp")
    body = functools.partial(per_device, mesh.shape["blk"], mesh.shape["tp"])
    return jax.shard_map(body, mesh=mesh, in_specs=in_specs, out_specs=out_specs, check_vma=False)
```

time: 71.3 us -> 50.3 us (0.71)
  Pallas kernels: 68.7 us -> 49.1 us
  local copies, waits for them, and re-layouts: 2.46 us -> 1.06 us
    pallas_call x1, Pallas kernels: 68.7 us -> 49.1 us  [per_device(): pl.pallas_call(functools.partial(kernel, n_blk, n_tp), out_shape=pltpu.VM...]
    unnamed x1, local copies, waits for them, and re-layouts: 2.46 us -> 1.06 us
where the time goes in v2:
time: 50.3 us; the launch traced here: 50.2 us
  Pallas kernels  49.1 us (98%)
  local copies, waits for them, and re-layouts  1.06 us (2%)
    pallas_call x1, Pallas kernels, per_device(): pl.pallas_call(functools.partial(kernel, n_blk, n_tp), out_shape=pltpu.VM...  49.1 us
    unnamed x1, local copies, waits for them, and re-layouts  1.06 us

profile of v2, /device:TPU:0, one launch (start us, length us, event | category | flops | bytes accessed | tf_op | source)
XLA Modules:
  0.0 50.2 jit_solution(9297611186723548541)
XLA Ops:
  0.0 49.1 %shard_map.64 = bf16[256,2560]{1,0:T(8,128)(2,1)S(1)} custom-call(bf16[256,2560]{1,0:T(8,128)(2,1)} %x_hbm.1, f32[1,5120]{1,0:T(1,128)} %bitcast.1, bf16[5120,384]{1,0:T(8,128)(2,1)} %wq_hbm.1, bf16[384,5120]{1,0:T(8,128)(2,1)} %wo_hbm.1, bf16[384,384]{1,0:T(8,128)(2,1)} %k_hbm.1, bf16[384,384]{1,0:T(8,128)(2,1)} %v_hbm.1), custom_call_target="tpu_custom_call" | custom-call | tf_op jit(solution)/shard_map/pallas_call | solution.py:470
  49.1 1.1 %copy.8 = bf16[256,2560]{1,0:T(8,128)(2,1)} copy(bf16[256,2560]{1,0:T(8,128)(2,1)S(1)} %shard_map.64) | data formatting | bytes 2621440

commit v3 on v2

--- a/solution.py
+++ b/solution.py
@@ -98,6 +98,11 @@
     def mate_index(m):
         return index(2 * m + par, side, core)
 
+    def parts_of(h):
+        if h < last:
+            return [(h, slice(0, rows))]
+        return [(h, slice(0, rows // 2)), (h + 1, slice(rows // 2, rows))]
+
     def ds(start, size, mult=LANES):
         return pl.ds(pl.multiple_of(start, mult), size)
 
@@ -242,8 +247,14 @@
             qsend[p, h] = jnp.dot(
                 xg[...], wq[p, h], preferred_element_type=jnp.float32
             ).astype(jnp.bfloat16)
-            place = head_recv.at[0, n_peer - 1 - j, h]
-            remote(qsend.at[p, h], qrecv.at[t, h], 3, place, {"tp": p}).start()
+            for place, part in parts_of(h):
+                remote(
+                    qsend.at[p, h, part],
+                    qrecv.at[t, h, part],
+                    3,
+                    head_recv.at[0, n_peer - 1 - j, place],
+                    {"tp": p},
+                ).start()
 
     tile = column_tile(feat)
 
@@ -273,81 +284,112 @@
         scale = math.log2(math.e) / math.sqrt(HEAD_DIM)
         fbuf[...] = lax.rsqrt(column / (feat * n_tp) + NORM_EPS) * scale
 
-    def mate_send(k, src, dst, h, i):
-        place = mate_recv.at[k, h, n_mate - 1 - i]
-        remote(src, dst, 5 + k, place, {"blk": mate_index(mates[i])}).start()
-
-    def q_make(h):
-        summed = own_part[:, head_cols(h)]
-        for j, p in enumerate(peers):
-            arrived(qrecv.at[p, h], head_recv.at[0, j, h])
-            summed = summed + qrecv[p, h].astype(jnp.float32)
-        qbuf[h] = (summed * fbuf[...]).astype(jnp.bfloat16)
+    def mate_send(k, src, dst, place, i):
+        there = mate_recv.at[k, place, n_mate - 1 - i]
+        remote(src, dst, 5 + k, there, {"blk": mate_index(mates[i])}).start()
+
+    def q_make(h, b):
+        place, part = parts_of(h)[b]
+        summed = own_part[part, head_cols(h)]
+        for j, p in enumerate(peers):
+            arrived(qrecv.at[p, h, part], head_recv.at[0, j, place])
+            summed = summed + qrecv[p, h, part].astype(jnp.float32)
+        qbuf[h, part] = (summed * fbuf[part]).astype(jnp.bfloat16)
         for i in range(n_mate):
-            mate_send(0, qbuf.at[h], qmate.at[h, pair], h, i)
-
-    def attend(h, query):
-        scores = []
-        for i in range(4):
-            keys = kvbuf[2 * h, 2 * i : 2 * i + 2].reshape(-1, HEAD_DIM)
-            scores.append(
-                lax.dot_general(
-                    query, keys, (((1,), (1,)), ((), ())), preferred_element_type=jnp.float32
+            mate_send(0, qbuf.at[h, part], qmate.at[h, pair, part], place, i)
+
+    def attend(h, query, emit):
+        half = rows // 2
+
+        def score(b):
+            block = query(b, slice(b * half, b * half + half))
+            scores = []
+            for i in range(4):
+                keys = kvbuf[2 * h, 2 * i : 2 * i + 2].reshape(-1, HEAD_DIM)
+                scores.append(
+                    lax.dot_general(
+                        block, keys, (((1,), (1,)), ((), ())), preferred_element_type=jnp.float32
+                    )
                 )
-            )
-        top = scores[0]
-        for s in scores[1:]:
-            top = jnp.maximum(top, s)
-        top = jnp.max(top, axis=1, keepdims=True)
-        mixed = jnp.zeros((rows, 2 * HEAD_DIM), jnp.float32)
-        for i in range(4):
-            vals = kvbuf[2 * h + 1, 2 * i : 2 * i + 2].reshape(-1, HEAD_DIM)
-            wide = jnp.concatenate([vals, jnp.ones_like(vals)], axis=1)
-            weights = jnp.exp2(scores[i] - top).astype(jnp.bfloat16)
-            mixed = mixed + jnp.dot(weights, wide, preferred_element_type=jnp.float32)
-        total = mixed[:, HEAD_DIM:]
-        return mixed[:, :HEAD_DIM] / total, top + jnp.log(total) * math.log2(math.e)
+            return scores
+
+        later = score(0)
+        for b in range(2):
+            scores = later
+            if b == 0:
+                later = score(1)
+            top = scores[0]
+            for s in scores[1:]:
+                top = jnp.maximum(top, s)
+            top = jnp.max(top, axis=1, keepdims=True)
+            mixed = jnp.zeros((half, 2 * HEAD_DIM), jnp.float32)
+            for i in range(4):
+                vals = kvbuf[2 * h + 1, 2 * i : 2 * i + 2].reshape(-1, HEAD_DIM)
+                wide = jnp.concatenate([vals, jnp.ones_like(vals)], axis=1)
+                weights = jnp.exp2(scores[i] - top).astype(jnp.bfloat16)
+                mixed = mixed + jnp.dot(weights, wide, preferred_element_type=jnp.float32)
+            total = mixed[:, HEAD_DIM:]
+            lse = top + jnp.log(total) * math.log2(math.e)
+            emit(b, slice(b * half, b * half + half), mixed[:, :HEAD_DIM] / total, lse)
 
     def att_own(h):
-        opart[h], lse_own[h] = attend(h, qbuf[h])
+        def emit(b, part, out, lse):
+            opart[h, part] = out
+            lse_own[h, part] = lse
+
+        attend(h, lambda b, part: qbuf[h, part], emit)
 
     def att_mate(h):
         for i, m in enumerate(mates):
-            arrived(qmate.at[h, m], mate_recv.at[0, h, i])
-            out, lse = attend(h, qmate[h, m])
-            osend[h, m] = out.astype(jnp.bfloat16)
-            mate_send(1, osend.at[h, m], orecv.at[h, pair], h, i)
-            ssend[h, m] = jnp.transpose(lse)[0:8, :]
-            mate_send(2, ssend.at[h, m], srecv.at[h, pair], h, i)
-
-    def att_cols(p, h):
-        return att.at[:, ds(h * span + p * HEAD_DIM, HEAD_DIM)]
-
-    def merge(h):
-        parts = [opart[h]]
-        logs = [lse_own[h]]
+
+            def query(b, part):
+                if b < len(parts_of(h)):
+                    place, piece = parts_of(h)[b]
+                    arrived(qmate.at[h, m, piece], mate_recv.at[0, place, i])
+                return qmate[h, m, part]
+
+            def emit(b, part, out, lse):
+                osend[h, m, part] = out.astype(jnp.bfloat16)
+                ssend[h, m, :, part] = jnp.transpose(lse)[0:8, :]
+                if b == 1 or len(parts_of(h)) == 2:
+                    place, piece = parts_of(h)[min(b, len(parts_of(h)) - 1)]
+                    mate_send(1, osend.at[h, m, piece], orecv.at[h, pair, piece], place, i)
+                    here, there = ssend.at[h, m, :, piece], srecv.at[h, pair, :, piece]
+                    mate_send(2, here, there, place, i)
+
+            attend(h, query, emit)
+
+    def att_ref(p, h, part):
+        return att.at[part, ds(h * span + p * HEAD_DIM, HEAD_DIM)]
+
+    def merge(h, b):
+        place, part = parts_of(h)[b]
+        parts = [opart[h, part]]
+        logs = [lse_own[h, part]]
         for i, m in enumerate(mates):
-            arrived(orecv.at[h, m], mate_recv.at[1, h, i])
-            arrived(srecv.at[h, m], mate_recv.at[2, h, i])
-            parts.append(orecv[h, m].astype(jnp.float32))
-            logs.append(jnp.transpose(jnp.broadcast_to(srecv[h, m][0:1, :], (LANES, rows))))
+            arrived(srecv.at[h, m, :, part], mate_recv.at[2, place, i])
+            arrived(orecv.at[h, m, part], mate_recv.at[1, place, i])
+            parts.append(orecv[h, m, part].astype(jnp.float32))
+            stat = srecv[h, m, 0:1, part]
+            logs.append(jnp.transpose(jnp.broadcast_to(stat, (LANES, stat.shape[1]))))
         top = logs[0]
         for log in logs[1:]:
             top = jnp.maximum(top, log)
         shares = [jnp.exp2(log - top) for log in logs]
         total = shares[0]
         mixed = shares[0] * parts[0]
-        for share, part in zip(shares[1:], parts[1:]):
+        for share, piece in zip(shares[1:], parts[1:]):
             total = total + share
-            mixed = mixed + share * part
-        att[:, ds(h * span + t * HEAD_DIM, HEAD_DIM)] = (mixed / total).astype(jnp.bfloat16)
-        for j, p in enumerate(peers):
-            place = head_recv.at[1, n_peer - 1 - j, h]
-            remote(att_cols(t, h), att_cols(t, h), 4, place, {"tp": p}).start()
-
-    def att_wait(h):
-        for j, p in enumerate(peers):
-            arrived(att_cols(p, h), head_recv.at[1, j, h])
+            mixed = mixed + share * piece
+        att[part, ds(h * span + t * HEAD_DIM, HEAD_DIM)] = (mixed / total).astype(jnp.bfloat16)
+        for j, p in enumerate(peers):
+            there = head_recv.at[1, n_peer - 1 - j, place]
+            remote(att_ref(t, h, part), att_ref(t, h, part), 4, there, {"tp": p}).start()
+
+    def att_wait(h, b):
+        place, part = parts_of(h)[b]
+        for j, p in enumerate(peers):
+            arrived(att_ref(p, h, part), head_recv.at[1, j, place])
 
     def wo_ref(p, h, q):
         return wo.at[ds(h * span + p * HEAD_DIM + q * wo_rows, wo_rows, wo_rows)]
@@ -389,7 +431,7 @@
         wo_loaded()
         for h in range(last):
             wo_ready(h)
-            att_wait(h)
+            att_wait(h, 0)
         for start in starts:
             cols = slice(start, start + tile)
             oacc[:, cols] = jnp.dot(
@@ -407,43 +449,48 @@
         at(2.0 + 0.1 * h, wq_start, h)
         at(2.45 if h == 0 else 2.6 + 0.01 * h, kv_loaded, h)
         for e in (k, v):
-            at(2.5 + 0.01 * e if h == 0 else 12.0 + 0.01 * e, kv_line, e)
-            at(2.5 + 0.01 * e if h == 0 else 2.65 if h < last else 9.0, kv_side, e)
+            at(2.5 + 0.01 * e if h == 0 else 9.36 + 0.001 * e, kv_line, e)
+            at(2.5 + 0.01 * e if h == 0 else 2.65 if h < last else 7.05, kv_side, e)
             at(2.7 + 0.01 * e, kv_core, e)
-        at((6.5, 17.7, 21.9)[stage], kv_from_partner, k)
-        at((8.6, 19.8, 24.0)[stage], kv_from_partner, v)
-        at((8.7, 12.9, 21.3)[stage], kv_from_beside, k)
-        at((8.8, 13.0, 21.4)[stage], kv_from_beside, v)
-        at((15.0, 23.3, 26.9)[stage], kv_from_corner, k)
-        at((17.0, 24.6, 26.95)[stage], kv_from_corner, v)
+        at((4.9, 16.3, 20.5)[stage], kv_from_partner, k)
+        at((7.0, 18.1, 23.4)[stage], kv_from_partner, v)
+        at((7.1, 9.4, 20.6)[stage], kv_from_beside, k)
+        at((7.2, 10.8, 20.7)[stage], kv_from_beside, v)
+        at((12.6, 21.7, 26.7)[stage], kv_from_corner, k)
+        at((14.6, 24.0, 26.8)[stage], kv_from_corner, v)
         for sub in range(SUBS):
-            at((6.4, 9.9, 14.1)[stage] + 1.75 * sub, wq_pass, h, sub)
-            at((12.0, 15.6, 17.6)[stage] + (1.75 if h == last else 0.2) * sub, wq_relay, h, sub)
-            at(17.5 if stage == 0 and sub == 0 else 21.2 + 0.1 * h, wo_start, h, sub)
-            at((26.8, 29.1, 31.6)[stage], wo_pass, h, sub)
-            at((31.7, 35.2, 37.1)[stage], wo_relay, h, sub)
-        at((13.6, 17.2, 20.7)[stage], q_part, h)
-        at((19.8, 22.0, 24.5)[stage], q_make, h)
-        at((21.3, 26.98, 29.2)[stage], kv_ready, h)
-        at((21.4, 31.8, 33.5)[stage], att_own, h)
-        at((24.8, 27.0, 29.5)[stage], att_mate, h)
-        at((31.75, 35.0, 37.0)[stage], merge, h)
+            at((4.2, 7.6, 11.2)[stage] + 1.75 * sub, wq_pass, h, sub)
+            at((10.2, 14.2, 14.7)[stage] + (1.75 if h == last else 0.1) * sub, wq_relay, h, sub)
+            at(15.6 if stage == 0 and sub == 0 else 18.0 + 0.1 * h, wo_start, h, sub)
+            at((23.5, 27.7, 30.3)[stage], wo_pass, h, sub)
+            at((30.4, 32.0, 34.1)[stage], wo_relay, h, sub)
+        at((12.0, 15.5, 17.7)[stage], q_part, h)
+        at((17.9, 19.6, 20.9)[stage], q_make, h, 0)
+        at((18.1, 25.3, 27.75)[stage], kv_ready, h)
+        at((18.2, 26.9, 29.6)[stage], att_own, h)
+        at((22.0, 25.4, 27.8)[stage], att_mate, h)
+        at((30.35, 31.9, 33.2)[stage], merge, h, 0)
+    at(21.4, q_make, last, 1)
+    at(34.0, merge, last, 1)
     at(4.0, norm)
-    at(19.7, factor)
+    at(17.85, factor)
     at(37.5, project_most)
     for when, order, step, args in sorted(events, key=lambda event: event[:2]):
         with jax.named_scope("_".join([step.__name__] + [str(a) for a in args])):
             step(*args)
 
-    with jax.named_scope("tail_wait"):
-        wo_ready(last)
-        att_wait(last)
-    for start in starts:
-        cols = slice(start, start + tile)
-        result = oacc[:, cols] + jnp.dot(
-            att[:, last * span :], wo[last * span :, cols], preferred_element_type=jnp.float32
-        )
-        out_ref[:, cols] = result.astype(jnp.bfloat16)
+    wo_ready(last)
+    for b, (place, part) in enumerate(parts_of(last)):
+        with jax.named_scope(f"tail_wait_{b}"):
+            att_wait(last, b)
+        for start in starts:
+            cols = slice(start, start + tile)
+            result = oacc[part, cols] + jnp.dot(
+                att[part, last * span :],
+                wo[last * span :, cols],
+                preferred_element_type=jnp.float32,
+            )
+            out_ref[part, cols] = result.astype(jnp.bfloat16)
     with jax.named_scope("drain"):
         sent(kvbuf.at[:, 0:7], 0)
         if n_peer:
@@ -510,8 +557,8 @@
             dma((n_tp - 1, heads, 2 * SUBS)),
             dma((n_tp - 1, heads)),
             dma((n_tp - 1,)),
-            dma((2, n_tp - 1, heads)),
-            dma((3, heads, max(n_pair - 1, 1))),
+            dma((2, n_tp - 1, heads + 1)),
+            dma((3, heads + 1, max(n_pair - 1, 1))),
             dma((heads,)),
             dma((4,)),
         ],

time: 50.3 us -> 48.7 us (0.968)
  Pallas kernels: 49.1 us -> 47.4 us
    pallas_call x1, Pallas kernels: 49.1 us -> 47.4 us  [per_device(): pl.pallas_call(functools.partial(kernel, n_blk, n_tp), out_shape=pltpu.VM...]
where the time goes in v3:
time: 48.7 us; the launch traced here: 48.5 us
  Pallas kernels  47.4 us (97%)
  local copies, waits for them, and re-layouts  1.06 us (2%)
    pallas_call x1, Pallas kernels, per_device(): pl.pallas_call(functools.partial(kernel, n_blk, n_tp), out_shape=pltpu.VM...  47.4 us
    unnamed x1, local copies, waits for them, and re-layouts  1.06 us

profile of v3, /device:TPU:0, one launch (start us, length us, event | category | flops | bytes accessed | tf_op | source)
XLA Modules:
  0.0 48.5 jit_solution(13438010832877626028)
XLA Ops:
  0.0 47.4 %shard_map.64 = bf16[256,2560]{1,0:T(8,128)(2,1)S(1)} custom-call(bf16[256,2560]{1,0:T(8,128)(2,1)} %x_hbm.1, f32[1,5120]{1,0:T(1,128)} %bitcast.1, bf16[5120,384]{1,0:T(8,128)(2,1)} %wq_hbm.1, bf16[384,5120]{1,0:T(8,128)(2,1)} %wo_hbm.1, bf16[384,384]{1,0:T(8,128)(2,1)} %k_hbm.1, bf16[384,384]{1,0:T(8,128)(2,1)} %v_hbm.1), custom_call_target="tpu_custom_call" | custom-call | tf_op jit(solution)/shard_map/pallas_call | solution.py:517
  47.4 1.1 %copy.8 = bf16[256,2560]{1,0:T(8,128)(2,1)} copy(bf16[256,2560]{1,0:T(8,128)(2,1)S(1)} %shard_map.64) | data formatting | bytes 2621440

commit v4 on v3

--- a/solution.py
+++ b/solution.py
@@ -171,7 +171,7 @@
     from_partner = slot(1 - par, side, core)
     from_corner = slot(1 - par, 1 - side, core)
 
-    by_line = (2 * heads - 1,)
+    by_line = ()
 
     def kv_loaded(h):
         both = kvbuf.at[2 * h : 2 * h + 2, mine]
@@ -219,13 +219,12 @@
         ref = wq_ref(peers[j], h, c)
         remote(ref, ref, 1, wq_core_recv.at[j, h], {"blk": sibling}).start()
 
-    def wq_start(h):
-        for k in range(2 * SUBS if h == last else SUBS):
-            for j, p in enumerate(peers):
-                c = wq_chunk(par if k < SUBS else 1 - par, core, k % SUBS)
-                src = wq_hbm.at[ds(p * feat + c * wq_rows, wq_rows, 16), head_cols(h)]
-                place = wq_recv.at[n_peer - 1 - j, h, k]
-                remote(src, wq_ref(t, h, c), 1, place, {"tp": p}).start()
+    def wq_start(h, k):
+        for j, p in enumerate(peers):
+            c = wq_chunk(par if k < SUBS else 1 - par, core, k % SUBS)
+            src = wq_hbm.at[ds(p * feat + c * wq_rows, wq_rows, 16), head_cols(h)]
+            place = wq_recv.at[n_peer - 1 - j, h, k]
+            remote(src, wq_ref(t, h, c), 1, place, {"tp": p}).start()
 
     def wq_pass(h, sub):
         for j, p in enumerate(peers):
@@ -339,6 +338,13 @@
 
         attend(h, lambda b, part: qbuf[h, part], emit)
 
+    def o_send(h, b):
+        place, part = parts_of(h)[b]
+        for i, m in enumerate(mates):
+            mate_send(1, osend.at[h, m, part], orecv.at[h, pair, part], place, i)
+            here, there = ssend.at[h, m, :, part], srecv.at[h, pair, :, part]
+            mate_send(2, here, there, place, i)
+
     def att_mate(h):
         for i, m in enumerate(mates):
 
@@ -350,12 +356,9 @@
 
             def emit(b, part, out, lse):
                 osend[h, m, part] = out.astype(jnp.bfloat16)
-                ssend[h, m, :, part] = jnp.transpose(lse)[0:8, :]
-                if b == 1 or len(parts_of(h)) == 2:
-                    place, piece = parts_of(h)[min(b, len(parts_of(h)) - 1)]
-                    mate_send(1, osend.at[h, m, piece], orecv.at[h, pair, piece], place, i)
-                    here, there = ssend.at[h, m, :, piece], srecv.at[h, pair, :, piece]
-                    mate_send(2, here, there, place, i)
+                ssend[h, m, :, part] = jnp.transpose(lse)[0:1, :]
+                if h == last:
+                    o_send(h, b)
 
             attend(h, query, emit)
 
@@ -370,7 +373,7 @@
             arrived(srecv.at[h, m, :, part], mate_recv.at[2, place, i])
             arrived(orecv.at[h, m, part], mate_recv.at[1, place, i])
             parts.append(orecv[h, m, part].astype(jnp.float32))
-            stat = srecv[h, m, 0:1, part]
+            stat = srecv[h, m, :, part]
             logs.append(jnp.transpose(jnp.broadcast_to(stat, (LANES, stat.shape[1]))))
         top = logs[0]
         for log in logs[1:]:
@@ -397,23 +400,27 @@
     def wo_chunk(yy, cc, sub):
         return (yy * 2 + cc) * SUBS + sub
 
+    def wo_half(h):
+        return par if h == last else side
+
     def wo_start(h, sub):
-        q = wo_chunk(side, core, sub)
+        q = wo_chunk(wo_half(h), core, sub)
         for j, p in enumerate(peers):
             src = wo_hbm.at[ds(h * HEAD_DIM + q * wo_rows, wo_rows, wo_rows), ds(p * feat, feat)]
             place = wo_recv.at[n_peer - 1 - j, h, sub]
             remote(src, wo_ref(t, h, q), 8, place, {"tp": p}).start()
 
     def wo_pass(h, sub):
-        for j, p in enumerate(peers):
-            ref = wo_ref(p, h, wo_chunk(side, core, sub))
+        target = partner if h == last else beside
+        for j, p in enumerate(peers):
+            ref = wo_ref(p, h, wo_chunk(wo_half(h), core, sub))
             arrived(ref, wo_recv.at[j, h, sub])
-            remote(ref, ref, 8, wo_recv.at[j, h, SUBS + sub], {"blk": beside}).start()
+            remote(ref, ref, 8, wo_recv.at[j, h, SUBS + sub], {"blk": target}).start()
             remote(ref, ref, 8, wo_core_recv.at[j, h], {"blk": sibling}).start()
 
     def wo_relay(h, sub):
         for j, p in enumerate(peers):
-            ref = wo_ref(p, h, wo_chunk(1 - side, core, sub))
+            ref = wo_ref(p, h, wo_chunk(1 - wo_half(h), core, sub))
             arrived(ref, wo_recv.at[j, h, SUBS + sub])
             remote(ref, ref, 8, wo_core_recv.at[j, h], {"blk": sibling}).start()
 
@@ -427,16 +434,16 @@
 
     starts = range(0, feat, tile)
 
-    def project_most():
-        wo_loaded()
-        for h in range(last):
-            wo_ready(h)
-            att_wait(h, 0)
+    def project(h):
+        if h == 0:
+            wo_loaded()
+        wo_ready(h)
+        att_wait(h, 0)
         for start in starts:
             cols = slice(start, start + tile)
-            oacc[:, cols] = jnp.dot(
-                att[:, : last * span], wo[: last * span, cols], preferred_element_type=jnp.float32
-            )
+            block = slice(h * span, (h + 1) * span)
+            result = jnp.dot(att[:, block], wo[block, cols], preferred_element_type=jnp.float32)
+            oacc[:, cols] = result if h == 0 else oacc[:, cols] + result
 
     events = []
 
@@ -446,35 +453,38 @@
     for h in range(heads):
         k, v = 2 * h, 2 * h + 1
         stage = max(h - last + 2, 0)
-        at(2.0 + 0.1 * h, wq_start, h)
+        for piece in range(2 * SUBS if h == last else SUBS):
+            at(12.01 if piece >= 2 * SUBS - 1 else 2.0 + 0.1 * h, wq_start, h, piece)
         at(2.45 if h == 0 else 2.6 + 0.01 * h, kv_loaded, h)
         for e in (k, v):
-            at(2.5 + 0.01 * e if h == 0 else 9.36 + 0.001 * e, kv_line, e)
-            at(2.5 + 0.01 * e if h == 0 else 2.65 if h < last else 7.05, kv_side, e)
+            at((2.5 + 0.01 * e, 9.36, 14.25 if e == k else 16.55)[stage], kv_line, e)
+            at((2.5 + 0.01 * e, 2.65, 7.05)[stage], kv_side, e)
             at(2.7 + 0.01 * e, kv_core, e)
-        at((4.9, 16.3, 20.5)[stage], kv_from_partner, k)
-        at((7.0, 18.1, 23.4)[stage], kv_from_partner, v)
-        at((7.1, 9.4, 20.6)[stage], kv_from_beside, k)
-        at((7.2, 10.8, 20.7)[stage], kv_from_beside, v)
-        at((12.6, 21.7, 26.7)[stage], kv_from_corner, k)
-        at((14.6, 24.0, 26.8)[stage], kv_from_corner, v)
+        at((4.9, 16.2, 21.85)[stage], kv_from_partner, k)
+        at((7.0, 18.1, 24.6)[stage], kv_from_partner, v)
+        at((7.1, 9.4, 20.2)[stage], kv_from_beside, k)
+        at((7.2, 10.8, 20.3)[stage], kv_from_beside, v)
+        at((12.6, 22.6, 27.1)[stage], kv_from_corner, k)
+        at((14.6, 24.7, 28.2)[stage], kv_from_corner, v)
         for sub in range(SUBS):
             at((4.2, 7.6, 11.2)[stage] + 1.75 * sub, wq_pass, h, sub)
-            at((10.2, 14.2, 14.7)[stage] + (1.75 if h == last else 0.1) * sub, wq_relay, h, sub)
-            at(15.6 if stage == 0 and sub == 0 else 18.0 + 0.1 * h, wo_start, h, sub)
-            at((23.5, 27.7, 30.3)[stage], wo_pass, h, sub)
-            at((30.4, 32.0, 34.1)[stage], wo_relay, h, sub)
-        at((12.0, 15.5, 17.7)[stage], q_part, h)
-        at((17.9, 19.6, 20.9)[stage], q_make, h, 0)
-        at((18.1, 25.3, 27.75)[stage], kv_ready, h)
-        at((18.2, 26.9, 29.6)[stage], att_own, h)
-        at((22.0, 25.4, 27.8)[stage], att_mate, h)
-        at((30.35, 31.9, 33.2)[stage], merge, h, 0)
-    at(21.4, q_make, last, 1)
+            at((10.2, 14.2, 15.2)[stage] + (3.3 if h == last else 0.1) * sub, wq_relay, h, sub)
+            at(16.05 if stage == 0 and sub == 0 else 20.1 + 0.1 * h, wo_start, h, sub)
+            at(((25.0, 26.15), (28.3, 30.42), (30.43, 30.6))[stage][sub], wo_pass, h, sub)
+            at((30.9, 32.0, 34.1)[stage], wo_relay, h, sub)
+        at((12.0, 16.0, 20.0)[stage], q_part, h)
+        at((16.5, 20.1, 23.5)[stage], q_make, h, 0)
+        at((16.6, 25.9, 30.2)[stage], kv_ready, h)
+        at((16.7, 26.1, 30.5)[stage], att_own, h)
+        at((21.9, 27.2, 30.4)[stage], att_mate, h)
+        if h < last:
+            at(34.05 if h < last - 1 else 37.5, project, h)
+            at(24.5 if stage == 0 else 27.25, o_send, h, 0)
+        at((31.0, 31.9, 33.2)[stage], merge, h, 0)
+    at(23.6, q_make, last, 1)
     at(34.0, merge, last, 1)
     at(4.0, norm)
-    at(17.85, factor)
-    at(37.5, project_most)
+    at(16.45, factor)
     for when, order, step, args in sorted(events, key=lambda event: event[:2]):
         with jax.named_scope("_".join([step.__name__] + [str(a) for a in args])):
             step(*args)
@@ -543,8 +553,8 @@
             pltpu.VMEM((heads, n_pair, rows, HEAD_DIM), bf16),
             pltpu.VMEM((heads, n_pair, rows, HEAD_DIM), bf16),
             pltpu.VMEM((heads, n_pair, rows, HEAD_DIM), bf16),
-            pltpu.VMEM((heads, n_pair, 8, rows), f32),
-            pltpu.VMEM((heads, n_pair, 8, rows), f32),
+            pltpu.VMEM((heads, n_pair, 1, rows), f32),
+            pltpu.VMEM((heads, n_pair, 1, rows), f32),
             pltpu.VMEM((heads, rows, HEAD_DIM), f32),
             pltpu.VMEM((heads, rows, LANES), f32),
             pltpu.VMEM((rows, n_tp * width), bf16),

time: 48.7 us -> 47.4 us (0.973)
  Pallas kernels: 47.4 us -> 46.2 us
    pallas_call x1, Pallas kernels: 47.4 us -> 46.2 us  [per_device(): pl.pallas_call(functools.partial(kernel, n_blk, n_tp), out_shape=pltpu.VM...]
where the time goes in v4:
time: 47.4 us; the launch traced here: 47.3 us
  Pallas kernels  46.2 us (97%)
  local copies, waits for them, and re-layouts  1.06 us (2%)
    pallas_call x1, Pallas kernels, per_device(): pl.pallas_call(functools.partial(kernel, n_blk, n_tp), out_shape=pltpu.VM...  46.2 us
    unnamed x1, local copies, waits for them, and re-layouts  1.06 us

profile of v4, /device:TPU:0, one launch (start us, length us, event | category | flops | bytes accessed | tf_op | source)
XLA Modules:
  0.0 47.3 jit_solution(3569201904598860507)
XLA Ops:
  0.0 46.2 %shard_map.64 = bf16[256,2560]{1,0:T(8,128)(2,1)S(1)} custom-call(bf16[256,2560]{1,0:T(8,128)(2,1)} %x_hbm.1, f32[1,5120]{1,0:T(1,128)} %bitcast.1, bf16[5120,384]{1,0:T(8,128)(2,1)} %wq_hbm.1, bf16[384,5120]{1,0:T(8,128)(2,1)} %wo_hbm.1, bf16[384,384]{1,0:T(8,128)(2,1)} %k_hbm.1, bf16[384,384]{1,0:T(8,128)(2,1)} %v_hbm.1), custom_call_target="tpu_custom_call" | custom-call | tf_op jit(solution)/shard_map/pallas_call | solution.py:527
  46.2 1.1 %copy.8 = bf16[256,2560]{1,0:T(8,128)(2,1)} copy(bf16[256,2560]{1,0:T(8,128)(2,1)S(1)} %shard_map.64) | data formatting | bytes 2621440

commit v5 on v4

--- a/solution.py
+++ b/solution.py
@@ -171,8 +171,6 @@
     from_partner = slot(1 - par, side, core)
     from_corner = slot(1 - par, 1 - side, core)
 
-    by_line = ()
-
     def kv_loaded(h):
         both = kvbuf.at[2 * h : 2 * h + 2, mine]
         pltpu.make_async_copy(both, both, kv_local.at[h]).wait()
@@ -188,14 +186,11 @@
 
     def kv_from_partner(e):
         kv_wait(e, from_partner, 1)
-        if e not in by_line:
-            kv_send(e, from_partner, 2, beside)
+        kv_send(e, from_partner, 2, beside)
         kv_share(e, from_partner)
 
     def kv_from_beside(e):
         kv_wait(e, from_beside, 0)
-        if e in by_line:
-            kv_send(e, from_beside, 2, partner)
         kv_share(e, from_beside)
 
     def kv_from_corner(e):
@@ -357,8 +352,6 @@
             def emit(b, part, out, lse):
                 osend[h, m, part] = out.astype(jnp.bfloat16)
                 ssend[h, m, :, part] = jnp.transpose(lse)[0:1, :]
-                if h == last:
-                    o_send(h, b)
 
             attend(h, query, emit)
 
@@ -400,27 +393,24 @@
     def wo_chunk(yy, cc, sub):
         return (yy * 2 + cc) * SUBS + sub
 
-    def wo_half(h):
-        return par if h == last else side
-
-    def wo_start(h, sub):
-        q = wo_chunk(wo_half(h), core, sub)
+    def wo_start(h, k):
+        q = wo_chunk(side if k < SUBS else 1 - side, core, k % SUBS)
         for j, p in enumerate(peers):
             src = wo_hbm.at[ds(h * HEAD_DIM + q * wo_rows, wo_rows, wo_rows), ds(p * feat, feat)]
-            place = wo_recv.at[n_peer - 1 - j, h, sub]
+            place = wo_recv.at[n_peer - 1 - j, h, k]
             remote(src, wo_ref(t, h, q), 8, place, {"tp": p}).start()
 
     def wo_pass(h, sub):
-        target = partner if h == last else beside
-        for j, p in enumerate(peers):
-            ref = wo_ref(p, h, wo_chunk(wo_half(h), core, sub))
+        for j, p in enumerate(peers):
+            ref = wo_ref(p, h, wo_chunk(side, core, sub))
             arrived(ref, wo_recv.at[j, h, sub])
-            remote(ref, ref, 8, wo_recv.at[j, h, SUBS + sub], {"blk": target}).start()
+            if h != last:
+                remote(ref, ref, 8, wo_recv.at[j, h, SUBS + sub], {"blk": beside}).start()
             remote(ref, ref, 8, wo_core_recv.at[j, h], {"blk": sibling}).start()
 
     def wo_relay(h, sub):
         for j, p in enumerate(peers):
-            ref = wo_ref(p, h, wo_chunk(1 - wo_half(h), core, sub))
+            ref = wo_ref(p, h, wo_chunk(1 - side, core, sub))
             arrived(ref, wo_recv.at[j, h, SUBS + sub])
             remote(ref, ref, 8, wo_core_recv.at[j, h], {"blk": sibling}).start()
 
@@ -466,25 +456,27 @@
         at((7.2, 10.8, 20.3)[stage], kv_from_beside, v)
         at((12.6, 22.6, 27.1)[stage], kv_from_corner, k)
         at((14.6, 24.7, 28.2)[stage], kv_from_corner, v)
+        for piece in range(2 * SUBS if h == last else SUBS):
+            at(16.05 if stage == 0 else 20.1 + 0.1 * h, wo_start, h, piece)
         for sub in range(SUBS):
             at((4.2, 7.6, 11.2)[stage] + 1.75 * sub, wq_pass, h, sub)
             at((10.2, 14.2, 15.2)[stage] + (3.3 if h == last else 0.1) * sub, wq_relay, h, sub)
-            at(16.05 if stage == 0 and sub == 0 else 20.1 + 0.1 * h, wo_start, h, sub)
-            at(((25.0, 26.15), (28.3, 30.42), (30.43, 30.6))[stage][sub], wo_pass, h, sub)
-            at((30.9, 32.0, 34.1)[stage], wo_relay, h, sub)
+            at(((25.0, 26.15), (28.25, 28.3), (30.43, 30.6))[stage][sub], wo_pass, h, sub)
+            at((30.9, 34.03, 34.2)[stage], wo_relay, h, sub)
         at((12.0, 16.0, 20.0)[stage], q_part, h)
-        at((16.5, 20.1, 23.5)[stage], q_make, h, 0)
+        at((15.5, 20.1, 23.5)[stage], q_make, h, 0)
         at((16.6, 25.9, 30.2)[stage], kv_ready, h)
         at((16.7, 26.1, 30.5)[stage], att_own, h)
         at((21.9, 27.2, 30.4)[stage], att_mate, h)
         if h < last:
             at(34.05 if h < last - 1 else 37.5, project, h)
-            at(24.5 if stage == 0 else 27.25, o_send, h, 0)
+        for b in range(len(parts_of(h))):
+            at((24.5, 27.25, 30.4)[stage], o_send, h, b)
         at((31.0, 31.9, 33.2)[stage], merge, h, 0)
     at(23.6, q_make, last, 1)
     at(34.0, merge, last, 1)
     at(4.0, norm)
-    at(16.45, factor)
+    at(15.45, factor)
     for when, order, step, args in sorted(events, key=lambda event: event[:2]):
         with jax.named_scope("_".join([step.__name__] + [str(a) for a in args])):
             step(*args)

time: 47.4 us -> 46.9 us (0.989)
  Pallas kernels: 46.2 us -> 45.7 us
    pallas_call x1, Pallas kernels: 46.2 us -> 45.7 us  [per_device(): pl.pallas_call(functools.partial(kernel, n_blk, n_tp), out_shape=pltpu.VM...]
where the time goes in v5:
time: 46.9 us; the launch traced here: 46.7 us
  Pallas kernels  45.7 us (97%)
  local copies, waits for them, and re-layouts  1.06 us (2%)
    pallas_call x1, Pallas kernels, per_device(): pl.pallas_call(functools.partial(kernel, n_blk, n_tp), out_shape=pltpu.VM...  45.7 us
    unnamed x1, local copies, waits for them, and re-layouts  1.06 us

profile of v5, /device:TPU:0, one launch (start us, length us, event | category | flops | bytes accessed | tf_op | source)
XLA Modules:
  0.0 46.7 jit_solution(15514061266837793175)
XLA Ops:
  0.0 45.7 %shard_map.64 = bf16[256,2560]{1,0:T(8,128)(2,1)S(1)} custom-call(bf16[256,2560]{1,0:T(8,128)(2,1)} %x_hbm.1, f32[1,5120]{1,0:T(1,128)} %bitcast.1, bf16[5120,384]{1,0:T(8,128)(2,1)} %wq_hbm.1, bf16[384,5120]{1,0:T(8,128)(2,1)} %wo_hbm.1, bf16[384,384]{1,0:T(8,128)(2,1)} %k_hbm.1, bf16[384,384]{1,0:T(8,128)(2,1)} %v_hbm.1), custom_call_target="tpu_custom_call" | custom-call | tf_op jit(solution)/shard_map/pallas_call | solution.py:519
  45.7 1.1 %copy.8 = bf16[256,2560]{1,0:T(8,128)(2,1)} copy(bf16[256,2560]{1,0:T(8,128)(2,1)S(1)} %shard_map.64) | data formatting | bytes 2621440

commit v6 on v5

--- a/solution.py
+++ b/solution.py
@@ -59,8 +59,6 @@
     kv_core_recv,
     wq_recv,
     wq_core_recv,
-    wo_recv,
-    wo_core_recv,
     sq_recv,
     head_recv,
     mate_recv,
@@ -397,22 +395,22 @@
         q = wo_chunk(side if k < SUBS else 1 - side, core, k % SUBS)
         for j, p in enumerate(peers):
             src = wo_hbm.at[ds(h * HEAD_DIM + q * wo_rows, wo_rows, wo_rows), ds(p * feat, feat)]
-            place = wo_recv.at[n_peer - 1 - j, h, k]
+            place = wq_recv.at[n_peer - 1 - j, h, k]
             remote(src, wo_ref(t, h, q), 8, place, {"tp": p}).start()
 
     def wo_pass(h, sub):
         for j, p in enumerate(peers):
             ref = wo_ref(p, h, wo_chunk(side, core, sub))
-            arrived(ref, wo_recv.at[j, h, sub])
-            if h != last:
-                remote(ref, ref, 8, wo_recv.at[j, h, SUBS + sub], {"blk": beside}).start()
-            remote(ref, ref, 8, wo_core_recv.at[j, h], {"blk": sibling}).start()
+            arrived(ref, wq_recv.at[j, h, sub])
+            if h != last or sub == 0:
+                remote(ref, ref, 8, wq_recv.at[j, h, SUBS + sub], {"blk": beside}).start()
+            remote(ref, ref, 8, wq_core_recv.at[j, h], {"blk": sibling}).start()
 
     def wo_relay(h, sub):
         for j, p in enumerate(peers):
             ref = wo_ref(p, h, wo_chunk(1 - side, core, sub))
-            arrived(ref, wo_recv.at[j, h, SUBS + sub])
-            remote(ref, ref, 8, wo_core_recv.at[j, h], {"blk": sibling}).start()
+            arrived(ref, wq_recv.at[j, h, SUBS + sub])
+            remote(ref, ref, 8, wq_core_recv.at[j, h], {"blk": sibling}).start()
 
     def wo_loaded():
         ref = wo.at[0:width]
@@ -420,7 +418,7 @@
 
     def wo_ready(h):
         for j in range(n_peer):
-            arrived(wo.at[0 : HEAD_DIM // 2], wo_core_recv.at[j, h])
+            arrived(wo.at[0 : HEAD_DIM // 2], wq_core_recv.at[j, h])
 
     starts = range(0, feat, tile)
 
@@ -457,7 +455,8 @@
         at((12.6, 22.6, 27.1)[stage], kv_from_corner, k)
         at((14.6, 24.7, 28.2)[stage], kv_from_corner, v)
         for piece in range(2 * SUBS if h == last else SUBS):
-            at(16.05 if stage == 0 else 20.1 + 0.1 * h, wo_start, h, piece)
+            if piece != SUBS:
+                at((16.05, 20.2, 23.65)[stage], wo_start, h, piece)
         for sub in range(SUBS):
             at((4.2, 7.6, 11.2)[stage] + 1.75 * sub, wq_pass, h, sub)
             at((10.2, 14.2, 15.2)[stage] + (3.3 if h == last else 0.1) * sub, wq_relay, h, sub)
@@ -556,8 +555,6 @@
             dma((heads,)),
             dma((n_tp - 1, heads, 2 * SUBS)),
             dma((n_tp - 1, heads)),
-            dma((n_tp - 1, heads, 2 * SUBS)),
-            dma((n_tp - 1, heads)),
             dma((n_tp - 1,)),
             dma((2, n_tp - 1, heads + 1)),
             dma((3, heads + 1, max(n_pair - 1, 1))),

time: 46.9 us -> 46.7 us (level)
  no operation moved by 1% of the time
where the time goes in v6:
time: 46.7 us; the launch traced here: 46.6 us
  Pallas kernels  45.5 us (97%)
  local copies, waits for them, and re-layouts  1.06 us (2%)
    pallas_call x1, Pallas kernels, per_device(): pl.pallas_call(functools.partial(kernel, n_blk, n_tp), out_shape=pltpu.VM...  45.5 us
    unnamed x1, local copies, waits for them, and re-layouts  1.06 us

profile of v6, /device:TPU:0, one launch (start us, length us, event | category | flops | bytes accessed | tf_op | source)
XLA Modules:
  0.0 46.6 jit_solution(5664114803054801509)
XLA Ops:
  0.0 45.5 %shard_map.64 = bf16[256,2560]{1,0:T(8,128)(2,1)S(1)} custom-call(bf16[256,2560]{1,0:T(8,128)(2,1)} %x_hbm.1, f32[1,5120]{1,0:T(1,128)} %bitcast.1, bf16[5120,384]{1,0:T(8,128)(2,1)} %wq_hbm.1, bf16[384,5120]{1,0:T(8,128)(2,1)} %wo_hbm.1, bf16[384,384]{1,0:T(8,128)(2,1)} %k_hbm.1, bf16[384,384]{1,0:T(8,128)(2,1)} %v_hbm.1), custom_call_target="tpu_custom_call" | custom-call | tf_op jit(solution)/shard_map/pallas_call | solution.py:518
  45.5 1.1 %copy.8 = bf16[256,2560]{1,0:T(8,128)(2,1)} copy(bf16[256,2560]{1,0:T(8,128)(2,1)S(1)} %shard_map.64) | data formatting | bytes 2621440

commit v7 on v6

--- a/solution.py
+++ b/solution.py
@@ -244,7 +244,7 @@
                     qsend.at[p, h, part],
                     qrecv.at[t, h, part],
                     3,
-                    head_recv.at[0, n_peer - 1 - j, place],
+                    head_recv.at[n_peer - 1 - j, place],
                     {"tp": p},
                 ).start()
 
@@ -284,7 +284,7 @@
         place, part = parts_of(h)[b]
         summed = own_part[part, head_cols(h)]
         for j, p in enumerate(peers):
-            arrived(qrecv.at[p, h, part], head_recv.at[0, j, place])
+            arrived(qrecv.at[p, h, part], head_recv.at[j, place])
             summed = summed + qrecv[p, h, part].astype(jnp.float32)
         qbuf[h, part] = (summed * fbuf[part]).astype(jnp.bfloat16)
         for i in range(n_mate):
@@ -377,13 +377,13 @@
             mixed = mixed + share * piece
         att[part, ds(h * span + t * HEAD_DIM, HEAD_DIM)] = (mixed / total).astype(jnp.bfloat16)
         for j, p in enumerate(peers):
-            there = head_recv.at[1, n_peer - 1 - j, place]
+            there = head_recv.at[n_peer - 1 - j, place]
             remote(att_ref(t, h, part), att_ref(t, h, part), 4, there, {"tp": p}).start()
 
     def att_wait(h, b):
         place, part = parts_of(h)[b]
         for j, p in enumerate(peers):
-            arrived(att_ref(p, h, part), head_recv.at[1, j, place])
+            arrived(att_ref(p, h, part), head_recv.at[j, place])
 
     def wo_ref(p, h, q):
         return wo.at[ds(h * span + p * HEAD_DIM + q * wo_rows, wo_rows, wo_rows)]
@@ -481,6 +481,17 @@
             step(*args)
 
     wo_ready(last)
+    with jax.named_scope("drain"):
+        sent(kvbuf.at[:, 0:7], 0)
+        if n_peer:
+            sent(wq.at[0:n_peer], 1)
+            sent(sqbuf.at[0:n_peer], 2)
+            sent(qsend.at[0:n_peer], 3)
+            sent(wo.at[0 : n_peer * width], 8)
+        if n_mate:
+            sent(qmate.at[:, 0:n_mate], 5)
+            sent(osend.at[:, 0:n_mate], 6)
+            sent(ssend.at[:, 0:n_mate], 7)
     for b, (place, part) in enumerate(parts_of(last)):
         with jax.named_scope(f"tail_wait_{b}"):
             att_wait(last, b)
@@ -492,18 +503,8 @@
                 preferred_element_type=jnp.float32,
             )
             out_ref[part, cols] = result.astype(jnp.bfloat16)
-    with jax.named_scope("drain"):
-        sent(kvbuf.at[:, 0:7], 0)
-        if n_peer:
-            sent(wq.at[0:n_peer], 1)
-            sent(sqbuf.at[0:n_peer], 2)
-            sent(qsend.at[0:n_peer], 3)
-            sent(qsend.at[0:n_peer], 4)
-            sent(wo.at[0 : n_peer * width], 8)
-        if n_mate:
-            sent(qmate.at[:, 0:n_mate], 5)
-            sent(osend.at[:, 0:n_mate], 6)
-            sent(ssend.at[:, 0:n_mate], 7)
+    if n_peer:
+        sent(qsend.at[0:n_peer], 4)
 
 
 def per_device(n_blk, n_tp, dec_states, norm_gain, query_weight, out_weight, enc_keys, enc_values):
@@ -556,7 +557,7 @@
             dma((n_tp - 1, heads, 2 * SUBS)),
             dma((n_tp - 1, heads)),
             dma((n_tp - 1,)),
-            dma((2, n_tp - 1, heads + 1)),
+            dma((n_tp - 1, heads + 1)),
             dma((3, heads + 1, max(n_pair - 1, 1))),
             dma((heads,)),
             dma((4,)),

time: 46.7 us -> 46.7 us (level)
  no operation moved by 1% of the time
where the time goes in v7:
time: 46.7 us; the launch traced here: 46.5 us
  Pallas kernels  45.5 us (97%)
  local copies, waits for them, and re-layouts  1.06 us (2%)
    pallas_call x1, Pallas kernels, per_device(): pl.pallas_call(functools.partial(kernel, n_blk, n_tp), out_shape=pltpu.VM...  45.5 us
    unnamed x1, local copies, waits for them, and re-layouts  1.06 us

profile of v7, /device:TPU:0, one launch (start us, length us, event | category | flops | bytes accessed | tf_op | source)
XLA Modules:
  0.0 46.5 jit_solution(15911823299114629167)
XLA Ops:
  0.0 45.5 %shard_map.64 = bf16[256,2560]{1,0:T(8,128)(2,1)S(1)} custom-call(bf16[256,2560]{1,0:T(8,128)(2,1)} %x_hbm.1, f32[1,5120]{1,0:T(1,128)} %bitcast.1, bf16[5120,384]{1,0:T(8,128)(2,1)} %wq_hbm.1, bf16[384,5120]{1,0:T(8,128)(2,1)} %wo_hbm.1, bf16[384,384]{1,0:T(8,128)(2,1)} %k_hbm.1, bf16[384,384]{1,0:T(8,128)(2,1)} %v_hbm.1), custom_call_target="tpu_custom_call" | custom-call | tf_op jit(solution)/shard_map/pallas_call | solution.py:519
  45.5 1.1 %copy.8 = bf16[256,2560]{1,0:T(8,128)(2,1)} copy(bf16[256,2560]{1,0:T(8,128)(2,1)S(1)} %shard_map.64) | data formatting | bytes 2621440
